TPU v7x, 32 devices: a whole 2x2x4 slice. The times are simulated.
32 devices in a mesh: dp: 8 (over z, y), mp: 4 (over x, core).
Axes of the slice: x: 2, y: 2, z: 4, core: 2. Of those that a mesh axis runs over, the one named last changes fastest.
Arguments:
- clip_feats: bfloat16 [8192, 768], P('dp'), may hold values from -6 to 6
- counts: int32 [8], P('dp'), may hold values from 102 to 1024, as said below
- gain_one: bfloat16 [768], replicated, may hold values from 0.5 to 1.5
- shift_one: bfloat16 [768], replicated, may hold values from -1 to 1
- q_weight: bfloat16 [768, 768], P(None, 'mp'), may hold values from -0.21875 to 0.21875
- k_weight: bfloat16 [768, 768], P(None, 'mp'), may hold values from -0.21875 to 0.21875
- v_weight: bfloat16 [768, 768], P(None, 'mp'), may hold values from -0.21875 to 0.21875
- q_bias: bfloat16 [768], P('mp'), may hold values from -3 to 3
- v_bias: bfloat16 [768], P('mp'), may hold values from -0.59765625 to 0.59765625
- o_weight: bfloat16 [768, 768], P('mp'), may hold values from -1.75 to 1.75
- o_bias: bfloat16 [768], replicated, may hold values from -1.5 to 1.5
- gain_two: bfloat16 [768], replicated, may hold values from 0.5 to 1.5
- shift_two: bfloat16 [768], replicated, may hold values from -1 to 1
- up_weight: bfloat16 [768, 3072], P(None, 'mp'), may hold values from -0.21875 to 0.21875
- up_bias: bfloat16 [3072], P('mp'), may hold values from -3 to 3
- down_weight: bfloat16 [3072, 768], P('mp'), may hold values from -0.109375 to 0.109375
- down_bias: bfloat16 [768], replicated, may hold values from -1.5 to 1.5
- out_grad: bfloat16 [8192, 768], P('dp'), may hold values from -6 to 6
Outputs:
- layer_out: bfloat16 [8192, 768], P(('dp', 'mp'))
- feats_grad: bfloat16 [8192, 768], P(('dp', 'mp'))
- gain_one_grad: float32 [768], P(('dp', 'mp'))
- shift_one_grad: float32 [768], P(('dp', 'mp'))
- q_weight_grad: float32 [768, 768], P('dp', 'mp')
- k_weight_grad: float32 [768, 768], P('dp', 'mp')
- v_weight_grad: float32 [768, 768], P('dp', 'mp')
- q_bias_grad: float32 [768], P(('mp', 'dp'))
- v_bias_grad: float32 [768], P(('mp', 'dp'))
- o_weight_grad: float32 [768, 768], P('mp', 'dp')
- o_bias_grad: float32 [768], P(('dp', 'mp'))
- gain_two_grad: float32 [768], P(('dp', 'mp'))
- shift_two_grad: float32 [768], P(('dp', 'mp'))
- up_weight_grad: float32 [768, 3072], P('dp', 'mp')
- up_bias_grad: float32 [3072], P(('mp', 'dp'))
- down_weight_grad: float32 [3072, 768], P('mp', 'dp')
- down_bias_grad: float32 [768], P(('dp', 'mp'))
Inputs may be any that keep to these rules, and one draw needn't show every extreme that they name: `counts`: the true patch count of each clip; some clip fills all 1024 slots.
All inputs are finite; a program needn't handle non-finite values.
Results may differ from a plain program's by a relative error of at most 0.02.
Values may be sent and summed in bfloat16 or wider, within the bound.
A program may use at most 128 MiB of HBM per device.

v0:
```python
import jax
import jax.numpy as jnp
from jax import lax
from jax.sharding import PartitionSpec as P

HD = 64


NORM_EPSILON = 1e-06
SCORE_SCALE = 0.125


def standardize(values):
    centered = values - jnp.mean(values, axis=-1, keepdims=True)
    variance = jnp.mean(centered * centered, axis=-1, keepdims=True)
    return centered * lax.rsqrt(variance + NORM_EPSILON)


def row_back(inputs, gain_vec, grad_rows):
    _, pull_back = jax.vjp(lambda values: standardize(values) * gain_vec, inputs)
    return pull_back(grad_rows)[0]


def product(left, right):
    return jnp.dot(left, right, preferred_element_type=jnp.float32)


def product_tn(left, right):
    return lax.dot_general(
        left, right, (((0,), (0,)), ((), ())), preferred_element_type=jnp.float32
    )


def product_nt(left, right):
    return lax.dot_general(
        left, right, (((1,), (1,)), ((), ())), preferred_element_type=jnp.float32
    )


def masked_scores(query_rows, key_clip, clip_len):
    scores = (
        jnp.einsum("qhd,khd->hqk", query_rows, key_clip, preferred_element_type=jnp.float32)
        * SCORE_SCALE
    )
    key_live = lax.broadcasted_iota(jnp.int32, (1, 1, key_clip.shape[0]), 2) < clip_len
    return jnp.where(key_live, scores, -1e30)


def attend_clip(pieces):
    query_clip, key_clip, value_clip, clip_len = pieces
    slot_count, head_count, head_size = query_clip.shape
    block_rows = min(512, slot_count)

    def one_block(query_rows):
        scores = masked_scores(query_rows, key_clip, clip_len)
        peak_score = jnp.max(scores, axis=-1, keepdims=True)
        exp_scores = jnp.exp(scores - peak_score)
        exp_total = jnp.sum(exp_scores, axis=-1, keepdims=True)
        probs = (exp_scores / exp_total).astype(jnp.bfloat16)
        mixed = jnp.einsum("hqk,khd->qhd", probs, value_clip, preferred_element_type=jnp.float32)
        return (mixed.astype(jnp.bfloat16), peak_score + jnp.log(exp_total))

    query_blocks = query_clip.reshape(slot_count // block_rows, block_rows, head_count, head_size)
    mixed, log_totals = lax.map(one_block, query_blocks)
    return (mixed.reshape(slot_count, head_count * head_size), log_totals)


def attend_back(pieces):
    query_clip, key_clip, value_clip, clip_len, log_totals, grad_clip = pieces
    slot_count, head_count, head_size = query_clip.shape
    block_rows = min(512, slot_count)
    block_shape = (slot_count // block_rows, block_rows, head_count, head_size)

    def one_block(carry, block_pieces):
        key_grad, value_grad = carry
        query_rows, log_rows, grad_rows = block_pieces
        probs = jnp.exp(masked_scores(query_rows, key_clip, clip_len) - log_rows)
        value_grad = value_grad + jnp.einsum(
            "hqk,qhd->khd",
            probs.astype(jnp.bfloat16),
            grad_rows,
            preferred_element_type=jnp.float32,
        )
        prob_grad = jnp.einsum(
            "qhd,khd->hqk", grad_rows, value_clip, preferred_element_type=jnp.float32
        )
        row_inner = jnp.sum(prob_grad * probs, axis=-1, keepdims=True)
        score_grad = (probs * (prob_grad - row_inner)).astype(jnp.bfloat16)
        query_grad = (
            jnp.einsum("hqk,khd->qhd", score_grad, key_clip, preferred_element_type=jnp.float32)
            * SCORE_SCALE
        )
        key_grad = (
            key_grad
            + jnp.einsum("hqk,qhd->khd", score_grad, query_rows, preferred_element_type=jnp.float32)
            * SCORE_SCALE
        )
        return ((key_grad, value_grad), query_grad)

    zeros_clip = jnp.zeros((slot_count, head_count, head_size), jnp.float32)
    (key_grad, value_grad), query_grad = lax.scan(
        one_block,
        (zeros_clip, zeros_clip),
        (query_clip.reshape(block_shape), log_totals, grad_clip.reshape(block_shape)),
    )
    width_here = head_count * head_size
    return (
        query_grad.reshape(slot_count, width_here).astype(jnp.bfloat16),
        key_grad.reshape(slot_count, width_here).astype(jnp.bfloat16),
        value_grad.reshape(slot_count, width_here).astype(jnp.bfloat16),
    )


def shards(
    clip_feats,
    counts,
    gain_one,
    shift_one,
    q_weight,
    k_weight,
    v_weight,
    q_bias,
    v_bias,
    o_weight,
    o_bias,
    gain_two,
    shift_two,
    up_weight,
    up_bias,
    down_weight,
    down_bias,
    out_grad,
):
    row_total = clip_feats.shape[0]
    clip_total = counts.shape[0]
    slot_count = row_total // clip_total
    share_rows = row_total // lax.axis_size("mp")
    share_start = lax.axis_index("mp") * share_rows
    head_count = q_weight.shape[1] // HD
    clip_shape = (clip_total, slot_count, head_count, HD)

    def mine(full_rows):
        return lax.dynamic_slice_in_dim(full_rows, share_start, share_rows, 0)

    feats = clip_feats.astype(jnp.float32)
    gain_one_f = gain_one.astype(jnp.float32)
    gain_two_f = gain_two.astype(jnp.float32)
    normed = (standardize(feats) * gain_one_f + shift_one.astype(jnp.float32)).astype(jnp.bfloat16)
    query = (product(normed, q_weight) + q_bias.astype(jnp.float32)).astype(jnp.bfloat16)
    keys_all = product(normed, k_weight).astype(jnp.bfloat16)
    values_all = (product(normed, v_weight) + v_bias.astype(jnp.float32)).astype(jnp.bfloat16)
    query_clips = query.reshape(clip_shape)
    key_clips = keys_all.reshape(clip_shape)
    value_clips = values_all.reshape(clip_shape)
    mixed, log_totals = lax.map(attend_clip, (query_clips, key_clips, value_clips, counts))
    mixed = mixed.reshape(row_total, head_count * HD)
    o_bias_f = o_bias.astype(jnp.float32)
    attn_full = (
        lax.psum(product(mixed, o_weight).astype(jnp.bfloat16), "mp").astype(jnp.float32) + o_bias_f
    )
    resid = feats + attn_full
    normed_two = (standardize(resid) * gain_two_f + shift_two.astype(jnp.float32)).astype(
        jnp.bfloat16
    )
    resid_mine = mine(resid)
    pre_up = product(normed_two, up_weight) + up_bias.astype(jnp.float32)
    hidden, gelu_back = jax.vjp(lambda values: jax.nn.gelu(values, approximate=False), pre_up)
    hidden = hidden.astype(jnp.bfloat16)
    mlp_mine = lax.psum_scatter(
        product(hidden, down_weight).astype(jnp.bfloat16), "mp", scatter_dimension=0, tiled=True
    ).astype(jnp.float32) + down_bias.astype(jnp.float32)
    layer_out = (resid_mine + mlp_mine).astype(jnp.bfloat16)
    row_live = (
        lax.broadcasted_iota(jnp.int32, (clip_total, slot_count), 1) < counts[:, None]
    ).reshape(row_total, 1)
    grad_full = jnp.where(row_live, out_grad.astype(jnp.float32), 0.0)
    grad_low = grad_full.astype(jnp.bfloat16)
    grad_mine = mine(grad_full)
    down_weight_grad = product_tn(hidden, grad_low)
    down_bias_grad = jnp.sum(grad_mine, axis=0)
    pre_grad = gelu_back(product_nt(grad_low, down_weight))[0].astype(jnp.bfloat16)
    up_weight_grad = product_tn(normed_two, pre_grad)
    up_bias_grad = jnp.sum(pre_grad, axis=0, dtype=jnp.float32)
    mlp_grads = (up_weight_grad, up_bias_grad, down_weight_grad)
    back_full = lax.psum(product_nt(pre_grad, up_weight).astype(jnp.bfloat16), "mp").astype(
        jnp.float32
    )
    resid_grad = grad_full + row_back(resid, gain_two_f, back_full)
    back_mine = mine(back_full)
    resid_grad_mine = mine(resid_grad)
    resid_low = resid_grad.astype(jnp.bfloat16)
    gain_two_grad = jnp.sum(back_mine * standardize(resid_mine), axis=0)
    shift_two_grad = jnp.sum(back_mine, axis=0)
    o_bias_grad = jnp.sum(mine(resid_low), axis=0, dtype=jnp.float32)
    o_weight_grad = product_tn(mixed, resid_low)
    mixed_grad = product_nt(resid_low, o_weight).astype(jnp.bfloat16)
    query_grad, key_grad, value_grad = lax.map(
        attend_back,
        (query_clips, key_clips, value_clips, counts, log_totals, mixed_grad.reshape(clip_shape)),
    )
    query_grad = query_grad.reshape(row_total, head_count * HD)
    key_grad = key_grad.reshape(row_total, head_count * HD)
    value_grad = value_grad.reshape(row_total, head_count * HD)
    q_weight_grad = product_tn(normed, query_grad)
    k_weight_grad = product_tn(normed, key_grad)
    v_weight_grad = product_tn(normed, value_grad)
    q_bias_grad = jnp.sum(query_grad, axis=0, dtype=jnp.float32)
    v_bias_grad = jnp.sum(value_grad, axis=0, dtype=jnp.float32)
    input_mine = lax.psum_scatter(
        (
            product_nt(query_grad, q_weight)
            + product_nt(key_grad, k_weight)
            + product_nt(value_grad, v_weight)
        ).astype(jnp.bfloat16),
        "mp",
        scatter_dimension=0,
        tiled=True,
    ).astype(jnp.float32)
    feats_mine = mine(feats)
    feats_grad = (resid_grad_mine + row_back(feats_mine, gain_one_f, input_mine)).astype(
        jnp.bfloat16
    )
    gain_one_grad = jnp.sum(input_mine * standardize(feats_mine), axis=0)
    shift_one_grad = jnp.sum(input_mine, axis=0)
    small_sums = (
        lax.psum_scatter(gain_one_grad, ("dp", "mp"), scatter_dimension=0, tiled=True),
        lax.psum_scatter(shift_one_grad, ("dp", "mp"), scatter_dimension=0, tiled=True),
        lax.psum_scatter(o_bias_grad, ("dp", "mp"), scatter_dimension=0, tiled=True),
        lax.psum_scatter(gain_two_grad, ("dp", "mp"), scatter_dimension=0, tiled=True),
        lax.psum_scatter(shift_two_grad, ("dp", "mp"), scatter_dimension=0, tiled=True),
        lax.psum_scatter(down_bias_grad, ("dp", "mp"), scatter_dimension=0, tiled=True),
    )
    every_sum = (
        lax.psum_scatter(q_weight_grad, "dp", scatter_dimension=0, tiled=True),
        lax.psum_scatter(k_weight_grad, "dp", scatter_dimension=0, tiled=True),
        lax.psum_scatter(v_weight_grad, "dp", scatter_dimension=0, tiled=True),
        lax.psum_scatter(q_bias_grad, "dp", scatter_dimension=0, tiled=True),
        lax.psum_scatter(v_bias_grad, "dp", scatter_dimension=0, tiled=True),
        lax.psum_scatter(o_weight_grad, "dp", scatter_dimension=1, tiled=True),
        lax.psum_scatter(up_weight_grad, "dp", scatter_dimension=0, tiled=True),
        lax.psum_scatter(up_bias_grad, "dp", scatter_dimension=0, tiled=True),
        lax.psum_scatter(down_weight_grad, "dp", scatter_dimension=1, tiled=True),
    )
    attn_sums = every_sum[:6]
    mlp_grads = every_sum[6:]
    return (
        layer_out,
        feats_grad,
        small_sums[0],
        small_sums[1],
        attn_sums[0],
        attn_sums[1],
        attn_sums[2],
        attn_sums[3],
        attn_sums[4],
        attn_sums[5],
        small_sums[2],
        small_sums[3],
        small_sums[4],
        mlp_grads[0],
        mlp_grads[1],
        mlp_grads[2],
        small_sums[5],
    )


def solution(mesh):
    placed = (
        P("dp", None),
        P("dp"),
        P(),
        P(),
        P(None, "mp"),
        P(None, "mp"),
        P(None, "mp"),
        P("mp"),
        P("mp"),
        P("mp", None),
        P(),
        P(),
        P(),
        P(None, "mp"),
        P("mp"),
        P("mp", None),
        P(),
        P("dp", None),
    )
    return jax.shard_map(
        shards,
        mesh=mesh,
        in_specs=placed,
        out_specs=(
            P(("dp", "mp"), None),
            P(("dp", "mp"), None),
            P(("dp", "mp")),
            P(("dp", "mp")),
            P("dp", "mp"),
            P("dp", "mp"),
            P("dp", "mp"),
            P(("mp", "dp")),
            P(("mp", "dp")),
            P("mp", "dp"),
            P(("dp", "mp")),
            P(("dp", "mp")),
            P(("dp", "mp")),
            P("dp", "mp"),
            P(("mp", "dp")),
            P("mp", "dp"),
            P(("dp", "mp")),
        ),
        check_vma=False,
    )
```

profile of v0, /device:TPU:0, one launch (start us, length us, event | category | flops | bytes accessed | tf_op | source)
XLA Modules:
  0.0 636.1 jit_solution(5282058169310767561)
XLA Ops:
  10.7 1.7 convert_reduce_fusion.1
  12.4 2.0 multiply_reduce_fusion.3
  17.3 2.1 convolution_convert_fusion.4
  19.4 2.9 fusion.49
  22.3 12.3 %while.47 = (s32[]{:T(128)}, bf16[2,512,3,64]{1,3,2,0:T(8,128)(2,1)}, f32[2,3,512,1]{2,1,3,0:T(4,128)S(1)}, s32[]{:T(128)}, bf16[2,512,3,64]{1,3,2,0:T(8,128)(2,...) while((s32[]{:T(128)}, bf16[2,512,3,64]{1,3,2,0:T(8,128)(2,1)}, ...), condition=%wide.region_5.6_spmd, body=%wide.region_2.5_spmd.sunk | while | flops 421625344 | bytes 24836288 | solution.py:64
  25.7 2.0 fusion.134
  31.9 2.0 fusion.134
  36.8 2.7 convolution_convert_fusion.2
  46.1 39.2 %all-reduce.14.cloned.1.call-done = bf16[1024,768]{1,0:T(8,128)(2,1)} async-done(((bf16[1024,768]{1,0:T(8,128)(2,1)}), bf16[1024,768]{1,0:T(8,128)(2,1)}) %all-reduce.14.cloned.1.call-update) | async-done | bytes 1572880 | tf_op jit(solution)/shard_map/psum | solution.py:159
  85.3 2.0 fusion.66
  88.6 9.4 %multiply_convert_fusion.1 = (bf16[1024,768]{1,0:T(8,128)(2,1)}, f32[1024,768]{1,0:T(8,128)S(1)}, f32[1024,768]{1,0:T(8,128)S(1)}) fusion(f32[768]{0:T(1024)S(1)} %copy-done.44, bf16[768,768]{1,0:T(8,128)(2,1)S(1)} %copy-done, f32[1024,768]{1,0:T(8,128)S(1)} %get-tuple-element.306, f32[768]{0:T(1024)S(1)} %copy-done.42, f32[768]{0:T(1024)S(1)} %copy-done.33, ...), kind=kOutput, calls=%fused_computation.58 | convolution fusion | flops 1263796224 | bytes 12207104 | tf_op jit(solution)/shard_map/dot_general | solution.py:25
  98.0 3.3 convert_reduce_fusion
  102.4 2.6 convolution_convert_fusion
  105.1 43.0 %all-reduce.16.cloned.1.call-done = bf16[1024,768]{1,0:T(8,128)(2,1)} async-done(((bf16[1024,768]{1,0:T(8,128)(2,1)}), bf16[1024,768]{1,0:T(8,128)(2,1)}) %all-reduce.16.cloned.1.call-update) | async-done | bytes 1572880 | tf_op jit(solution)/shard_map/psum | solution.py:185
  148.1 3.2 multiply_reduce_fusion.1
  151.4 2.9 fusion.63
  154.6 3.5 fusion.64
  159.3 1.7 convolution_bitcast_fusion
  161.1 4.3 convolution_convert_fusion.1
  165.7 2.8 convolution_convert_fusion.3
  168.6 2.1 reshape.207
  170.6 1.8 copy.46
  172.4 18.4 %while.48 = (s32[]{:T(128)}, f32[1024,3,64]{0,2,1:T(8,128)S(1)}, f32[1024,3,64]{0,2,1:T(8,128)}, bf16[2,512,3,64]{1,3,2,0:T(8,128)(2,1)}, bf16[2,512,3,64]{1,3,2...) while((s32[]{:T(128)}, f32[1024,3,64]{0,2,1:T(8,128)S(1)}, ...), condition=%wide.region_15.16_spmd.clone, body=%wide.region_13.15_spmd.clone.sunk | while | flops 1031306752 | bytes 63752492 | solution.py:101
  175.9 2.1 multiply_reduce_fusion.8
  178.0 1.7 multiply_convert_fusion.3
  185.1 2.1 multiply_reduce_fusion.8
  187.2 1.7 multiply_convert_fusion.3
  193.9 1.8 add_convert_fusion
  195.8 2.9 fusion.72
  198.8 2.9 fusion.71
  201.8 2.9 fusion.70
  205.1 5.5 fusion.67
  210.7 4.9 fusion.54
  215.7 1.9 convert_element_type.145
  223.7 21.7 %all-reduce.10 = (f32[192]{0:T(256)S(1)}, f32[192]{0:T(256)S(1)}, f32[768]{0:T(1024)S(1)}) all-reduce(f32[192]{0:T(256)S(1)} %reduce_sum.256, f32[192]{0:T(256)S(1)} %reduce_sum.258, f32[768]{0:T(1024)S(1)} %copy-done.41), channel_id=9, replica_groups=mesh['dp'=8,'mp'=4] {'dp'}, use_global_device_ids=true, to_apply=%region_29.30.clone | all-reduce | flops 1152 | bytes 9216
  247.1 1.9 convert_element_type.170
  250.4 1.7 copy.49
  252.2 1.8 reduce-scatter.11.cloned.1.call-done
  253.9 2.4 dynamic-slice_reduce_fusion.1
  256.4 28.0 %reduce-scatter.13.cloned.1.call-done = bf16[256,768]{1,0:T(8,128)(2,1)} async-done(((bf16[1024,768]{1,0:T(8,128)(2,1)}), bf16[256,768]{1,0:T(8,128)(2,1)}) %reduce-scatter.13.cloned.1.call-update) | async-done | bytes 393232 | tf_op jit(solution)/shard_map/reduce_scatter | solution.py:209
  286.0 1.7 fusion.53
  287.7 39.9 %all-reduce.9 = (f32[768]{0:T(1024)S(1)}, f32[768]{0:T(1024)S(1)}, f32[768]{0:T(1024)S(1)}, f32[768]{0:T(1024)S(1)}, f32[768]{0:T(1024)S(1)}, /*index=5*/f32[768]{0:T(1024)S(1)}) all-reduce(f32[768]{0:T(1024)S(1)} %get-tuple-element.249, f32[768]{0:T(1024)S(1)} %get-tuple-element.255, ...), channel_id=4, replica_groups=mesh['dp'=8,'mp'=4] {'dp','mp'}, use_global_device_ids=true, to_apply=%region_22.23.clone | all-reduce | flops 4608 | bytes 36864
  331.1 2.5 add_convert_fusion.4
  333.6 17.9 %reduce-scatter.19.cloned.1.call-done = f32[96,192]{1,0:T(8,128)} async-done(((f32[768,192]{1,0:T(8,128)}), f32[96,192]{1,0:T(8,128)}) %reduce-scatter.19.cloned.1.call-update) | async-done | bytes 73744 | tf_op jit(solution)/shard_map/reduce_scatter | solution.py:236
  351.5 66.1 %reduce-scatter.17.cloned.1.call-done = f32[96,192]{1,0:T(8,128)} async-done(((f32[768,192]{1,0:T(8,128)}), f32[96,192]{1,0:T(8,128)}) %reduce-scatter.17.cloned.1.call-update) | async-done | bytes 73744 | tf_op jit(solution)/shard_map/reduce_scatter | solution.py:235
  417.6 66.1 %reduce-scatter.15.cloned.1.call-done = f32[96,192]{1,0:T(8,128)} async-done(((f32[768,192]{1,0:T(8,128)}), f32[96,192]{1,0:T(8,128)}) %reduce-scatter.15.cloned.1.call-update) | async-done | bytes 73744 | tf_op jit(solution)/shard_map/reduce_scatter | solution.py:234
  483.7 72.8 %reduce-scatter.21.cloned.1.call-done = f32[96,768]{1,0:T(8,128)} async-done(((f32[768,768]{1,0:T(8,128)}), f32[96,768]{1,0:T(8,128)}) %reduce-scatter.21.cloned.1.call-update) | async-done | bytes 294928 | tf_op jit(solution)/shard_map/reduce_scatter | solution.py:240
  556.5 72.7 %reduce-scatter.23.cloned.1.call-done = f32[768,96]{0,1:T(8,128)} async-done(((f32[768,768]{0,1:T(8,128)}), f32[768,96]{0,1:T(8,128)}) %reduce-scatter.23.cloned.1.call-update) | async-done | bytes 294928 | tf_op jit(solution)/shard_map/reduce_scatter | solution.py:242
  (218 shorter events, 54.1 us)
Async XLA Ops:
  7.2 81.3 %copy-start = (bf16[768,768]{1,0:T(8,128)(2,1)S(1)}, bf16[768,768]{1,0:T(8,128)(2,1)}, u32[]{:S(2)}) copy-start(bf16[768,768]{1,0:T(8,128)(2,1)} %param.35) | copy-start | bytes 3538948
  7.2 7.2 %copy-start.4 = (bf16[1024,768]{1,0:T(8,128)(2,1)S(1)}, bf16[1024,768]{1,0:T(8,128)(2,1)}, u32[]{:S(2)}) copy-start(bf16[1024,768]{1,0:T(8,128)(2,1)} %param.22) | copy-start | bytes 4718596
  7.2 78.1 %all-reduce.14.cloned.1.call-start = ((), (), s32[]{:S(2)}) async-start(), calls=%async_computation.8 | async-start | bytes 3145728 | tf_op jit(solution)/shard_map/psum | solution.py:159
  10.0 5.1 copy-start.28
  10.7 5.6 copy-start.26
  39.6 108.5 %all-reduce.16.cloned.1.call-start = ((), (), s32[]{:S(2)}) async-start(), calls=%async_computation.10 | async-start | bytes 3145728 | tf_op jit(solution)/shard_map/psum | solution.py:185
  87.3 10.6 %copy-start.2 = (f32[1024,768]{1,0:T(8,128)}, f32[1024,768]{1,0:T(8,128)S(1)}, u32[]{:S(2)}) copy-start(f32[1024,768]{1,0:T(8,128)S(1)} %get-tuple-element.306) | copy-start | bytes 9437188
  87.4 10.6 %copy-start.30 = (f32[1024]{0:T(1024)}, f32[1024]{0:T(1024)S(1)}, u32[]{:S(2)}) copy-start(f32[1024]{0:T(1024)S(1)} %broadcast_multiply_fusion) | copy-start | bytes 12292
  88.5 9.4 %copy-start.38 = (f32[1024]{0:T(1024)}, f32[1024]{0:T(1024)S(1)}, u32[]{:S(2)}) copy-start(f32[1024]{0:T(1024)S(1)} %fusion.60) | copy-start | bytes 12292
  88.5 9.4 %copy-start.14 = (bf16[1024,768]{1,0:T(8,128)(2,1)S(1)}, bf16[1024,768]{1,0:T(8,128)(2,1)}, u32[]{:S(2)}) copy-start(bf16[1024,768]{1,0:T(8,128)(2,1)} %param.39) | copy-start | bytes 4718596
  88.6 9.4 %copy-start.46 = (pred[1024]{0:T(1024)(128)(4,1)S(1)}, pred[1024]{0:T(1024)(128)(4,1)}, u32[]{:S(2)}) copy-start(pred[1024]{0:T(1024)(128)(4,1)} %iota_compare_fusion.2) | copy-start | bytes 3076
  88.6 9.4 %copy-start.49 = (bf16[768,768]{1,0:T(8,128)(2,1)S(1)}, bf16[768,768]{1,0:T(8,128)(2,1)}, u32[]{:S(2)}) copy-start(bf16[768,768]{1,0:T(8,128)(2,1)} %param.37) | copy-start | bytes 3538948
  105.0 46.3 %copy-start.37 = (f32[1024]{0:T(1024)S(1)}, f32[1024]{0:T(1024)}, u32[]{:S(2)}) copy-start(f32[1024]{0:T(1024)} %copy-done.36) | copy-start | bytes 12292
  105.0 46.4 %copy-start.31 = (f32[1024]{0:T(1024)S(1)}, f32[1024]{0:T(1024)}, u32[]{:S(2)}) copy-start(f32[1024]{0:T(1024)} %copy-done.30) | copy-start | bytes 12292
  105.0 46.4 %copy-start.34 = (f32[768]{0:T(1024)S(1)}, f32[768]{0:T(1024)}, u32[]{:S(2)}) copy-start(f32[768]{0:T(1024)} %convert_element_type.157) | copy-start | bytes 9220
  105.0 46.4 %copy-start.39 = (f32[1024]{0:T(1024)S(1)}, f32[1024]{0:T(1024)}, u32[]{:S(2)}) copy-start(f32[1024]{0:T(1024)} %copy-done.38) | copy-start | bytes 12292
  105.0 145.4 %reduce-scatter.25.cloned.1.call-start = ((), (), s32[]{:S(2)}) async-start(), calls=%async_computation.17 | async-start | bytes 884736
  148.1 3.3 copy-start.5
  151.3 3.0 copy-start.3
  151.4 3.3 copy-start.15
  151.4 3.3 copy-start.47
  154.6 4.7 copy-start.13
  161.0 92.9 %reduce-scatter.11.cloned.1.call-start = ((), (), s32[]{:S(2)}) async-start(), calls=%async_computation.9 | async-start | bytes 1966080 | tf_op jit(solution)/shard_map/reduce_scatter | solution.py:169
  165.4 7.0 %copy-start.9 = (bf16[1024,3,64]{0,2,1:T(8,128)(2,1)S(1)}, bf16[1024,3,64]{0,2,1:T(8,128)(2,1)}, u32[]{:S(2)}) copy-start(bf16[1024,3,64]{0,2,1:T(8,128)(2,1)} %get-tuple-element.505) | copy-start | bytes 1179652
  165.5 118.9 %reduce-scatter.13.cloned.1.call-start = ((), (), s32[]{:S(2)}) async-start(), calls=%async_computation.11 | async-start | bytes 1966080 | tf_op jit(solution)/shard_map/reduce_scatter | solution.py:209
  175.9 2.1 copy-start.20
  178.0 1.7 copy-start.16
  185.1 2.1 copy-start.20
  187.2 1.7 copy-start.16
  190.9 1.8 copy-start.25
  190.9 2.4 copy-start.27
  195.7 155.8 %reduce-scatter.19.cloned.1.call-start = ((), (), s32[]{:S(2)}) async-start(), calls=%async_computation.14 | async-start | bytes 884736 | tf_op jit(solution)/shard_map/reduce_scatter | solution.py:236
  198.7 6.3 copy-start.32
  198.7 6.3 copy-start.35
  198.8 6.3 copy-start.40
  198.8 6.3 copy-start.43
  198.8 218.8 %reduce-scatter.17.cloned.1.call-start = ((), (), s32[]{:S(2)}) async-start(), calls=%async_computation.13 | async-start | bytes 884736 | tf_op jit(solution)/shard_map/reduce_scatter | solution.py:235
  201.8 281.9 %reduce-scatter.15.cloned.1.call-start = ((), (), s32[]{:S(2)}) async-start(), calls=%async_computation.12 | async-start | bytes 884736 | tf_op jit(solution)/shard_map/reduce_scatter | solution.py:234
  204.8 6.0 copy-start.48
  204.8 351.8 %reduce-scatter.21.cloned.1.call-start = ((), (), s32[]{:S(2)}) async-start(), calls=%async_computation.15 | async-start | bytes 2654208 | tf_op jit(solution)/shard_map/reduce_scatter | solution.py:240
  210.7 418.6 %reduce-scatter.23.cloned.1.call-start = ((), (), s32[]{:S(2)}) async-start(), calls=%async_computation.16 | async-start | bytes 2654208 | tf_op jit(solution)/shard_map/reduce_scatter | solution.py:242
  215.7 1.9 copy-start.50
  215.7 3.8 copy-start.45
  215.7 7.7 %copy-start.18 = (bf16[2,512,3,64]{1,3,2,0:T(8,128)(2,1)S(1)}, bf16[2,512,3,64]{1,3,2,0:T(8,128)(2,1)}, u32[]{:S(2)}) copy-start(bf16[2,512,3,64]{1,3,2,0:T(8,128)(2,1)} %get-tuple-element.162) | copy-start | bytes 1179652
  215.7 8.0 %copy-start.41 = (f32[768]{0:T(1024)S(1)}, f32[768]{0:T(1024)}, u32[]{:S(2)}) copy-start(f32[768]{0:T(1024)} %get-tuple-element.316) | copy-start | bytes 9220
  217.6 29.6 %copy-start.6 = (bf16[1024,768]{1,0:T(8,128)(2,1)S(1)}, bf16[1024,768]{1,0:T(8,128)(2,1)}, u32[]{:S(2)}) copy-start(bf16[1024,768]{1,0:T(8,128)(2,1)} %all-reduce.16.cloned.1.call-done) | copy-start | bytes 4718596
  247.1 37.3 %copy-start.29 = (f32[768]{0:T(1024)S(1)}, f32[768]{0:T(1024)}, u32[]{:S(2)}) copy-start(f32[768]{0:T(1024)} %copy-done.28) | copy-start | bytes 9220
  250.4 378.9 %copy-start.1 = (bf16[768,768]{1,0:T(8,128)(2,1)S(1)}, bf16[768,768]{1,0:T(8,128)(2,1)}, u32[]{:S(2)}) copy-start(bf16[768,768]{1,0:T(8,128)(2,1)} %param.35) | copy-start | bytes 3538948
  (22 other events, 25.5 us)
Sparse Core Ops, SparseCore 0:
  39.7 45.5 all-reduce.13
  105.2 42.9 all-reduce.15
  161.1 63.3 reduce-scatter.24
  227.0 26.9 reduce-scatter.10
  256.3 28.0 reduce-scatter.12
  288.1 63.3 reduce-scatter.18
  355.4 62.1 reduce-scatter.16
  421.5 62.1 reduce-scatter.14
  487.8 68.7 reduce-scatter.20
  560.5 68.7 reduce-scatter.22
where the time goes:
time: 637 us; the launch traced here: 636 us
  waiting for transfers between devices  408 us (64%)
  matrix products  73.9 us (12%)
  blocking collectives  61.5 us (10%)
  other arithmetic  52.5 us (8%)
  local copies, waits for them, and re-layouts  22.1 us (3%)
  between operations  16.8 us (3%)
    reduce_scatter x1, waiting for transfers between devices, shards(): lax.psum_scatter(up_weight_grad, 'dp', scatter_dimension=0, tiled=True)  72.8 us
    reduce_scatter x1, waiting for transfers between devices, shards(): lax.psum_scatter(down_weight_grad, 'dp', scatter_dimension=1, tiled=True)  72.7 us
    reduce_scatter x1, waiting for transfers between devices, shards(): lax.psum_scatter(q_weight_grad, 'dp', scatter_dimension=0, tiled=True)  66.1 us
    reduce_scatter x1, waiting for transfers between devices, shards(): lax.psum_scatter(k_weight_grad, 'dp', scatter_dimension=0, tiled=True)  66.1 us
    unnamed x2, blocking collectives  61.5 us
    psum x1, waiting for transfers between devices, shards(): lax.psum(product_nt(pre_grad, up_weight).astype(jnp.bfloat16), 'mp')  43 us
    psum x1, waiting for transfers between devices, shards(): lax.psum(product(mixed, o_weight).astype(jnp.bfloat16), 'mp')  39.2 us
    reduce_scatter x1, waiting for transfers between devices, shards(): lax.psum_scatter((product_nt(query_grad, q_weight) + product_nt(key_grad,...  28 us
  transfers between devices with their start and end apart: 10, of which 9 were waited for; matrix products, arithmetic and copies ran while one was open for 13% of the time, Pallas kernels for 0%

commit v1 on v0

v1 whole, which is shorter than its diff:
```python
import functools
import types

import jax
import jax.numpy as jnp
from jax import lax
from jax.experimental import pallas as pl
from jax.experimental.pallas import tpu as pltpu
from jax.sharding import PartitionSpec as P

HD = 64
NORM_EPSILON = 1e-06
SCORE_SCALE = 0.125
BLOCK = 256
MESH = pl.DeviceIdType.MESH
F32 = jnp.float32
BF16 = jnp.bfloat16
INV_SQRT2 = 0.7071067811865476
INV_SQRT_2PI = 0.3989422804014327
NEG = -1e30

PIECES = (("down", (0, 1, 2)), ("up", (1, 0, 2)), ("qk", (0, 1, 2)), ("vo", (1, 0, 2)))


def dot(left, right):
    return jnp.dot(left, right, preferred_element_type=F32)


def dot_nt(left, right):
    return lax.dot_general(left, right, (((1,), (1,)), ((), ())), preferred_element_type=F32)


def dot_tn(left, right):
    return lax.dot_general(left, right, (((0,), (0,)), ((), ())), preferred_element_type=F32)


def standardized(values):
    centered = values - jnp.mean(values, axis=-1, keepdims=True)
    variance = jnp.mean(centered * centered, axis=-1, keepdims=True)
    inverse = lax.rsqrt(variance + NORM_EPSILON)
    return centered * inverse, inverse


def norm_back(std_rows, inverse, gain, grad):
    scaled = gain * grad
    mean_scaled = jnp.mean(scaled, axis=-1, keepdims=True)
    mean_inner = jnp.mean(scaled * std_rows, axis=-1, keepdims=True)
    return inverse * (scaled - mean_scaled - std_rows * mean_inner)


def gelu_pair(values):
    bell = jnp.exp(-0.5 * (values * values))
    t = 1.0 / (1.0 + (0.3275911 * INV_SQRT2) * jnp.abs(values))
    tail = t * (0.127414796 + t * (-0.142248368 + t * (0.7107068705 + t * (-0.7265760135 + t * 0.5307027145)))) * bell
    phi = jnp.where(values >= 0.0, 1.0 - tail, tail)
    return values * phi, phi + values * (bell * INV_SQRT_2PI)


def column_sum(values):
    return jnp.sum(values, axis=0, keepdims=True)


def row_of(ref):
    return ref[...].astype(F32).reshape(1, -1)


def layer_kernel(names, dp_bits, *refs):
    r = types.SimpleNamespace(**dict(zip(names, refs)))
    rows, width = r.feats_hbm.shape
    cols = r.qw_hbm.shape[1]
    hidden_cols = r.up_hbm.shape[1]
    heads = cols // HD
    blocks = rows // BLOCK

    m = lax.axis_index("mp")
    c = m % 2
    x = m // 2
    cp = m + 1 - 2 * c
    xp = m + 2 - 4 * x
    count = r.counts[0]

    def bit_of(bit):
        return (lax.axis_index("dp") // (1 << bit)) % 2

    def dp_partner(bit):
        return lax.axis_index("dp") + (1 << bit) * (1 - 2 * bit_of(bit))

    loads = [
        ("feats_hbm", r.feats), ("qw_hbm", r.qw), ("kw_hbm", r.kw), ("vw_hbm", r.vw),
        ("ow_hbm", r.ow.at[pl.ds(pl.multiple_of(m * cols, 64), cols), :]), ("og_hbm", r.og),
        ("down_hbm", r.down), ("up_hbm", r.up),
    ]

    def load(i):
        return pltpu.make_async_copy(getattr(r, loads[i][0]), loads[i][1], r.load_sem.at[i])

    for i in range(len(loads)):
        load(i).start()

    barrier = pltpu.get_barrier_semaphore()
    partners = [{"mp": cp}, {"mp": xp}] + [{"dp": dp_partner(bit)} for bit in range(dp_bits)]
    for partner in partners:
        pl.semaphore_signal(barrier, inc=1, device_id=partner, device_id_type=MESH)
    pl.semaphore_wait(barrier, len(partners))

    def remote(index, source, target, partner):
        return pltpu.make_async_remote_copy(
            src_ref=source, dst_ref=target, send_sem=r.send_sem.at[index], recv_sem=r.recv_sem.at[index],
            device_id=partner, device_id_type=MESH,
        )

    def rows_at(start, size):
        return pl.ds(pl.multiple_of(start, size), size)

    OW, MX, RL, BK, ML, IN, SM = 0, 3, 12, 15, 18, 21, 24
    DP = SM + dp_bits + 2

    def ow_copy(kind):
        owner = (m, m, xp)[kind]
        view = r.ow.at[rows_at(owner * cols, 64 * 3), :]
        return remote(OW + kind, view, view, {"mp": (cp, xp, cp)[kind]})

    def mx_copy(kind, h):
        owner = (m, m, xp)[kind]
        view = r.mixed_t.at[rows_at(owner * cols + h * HD, HD), :]
        return remote(MX + kind * 3 + h, view, view, {"mp": (cp, xp, cp)[kind]})

    def rl_copy(kind):
        owner = (m, m, xp)[kind]
        view = r.resid_low.at[rows_at(owner * BLOCK, BLOCK), :]
        return remote(RL + kind, view, view, {"mp": (cp, xp, cp)[kind]})

    def rs_copy(base, step):
        send, receive = {BK: (r.bk_tx, r.bk_rx), ML: (r.ml_tx, r.ml_rx), IN: (r.in_tx, r.in_rx)}[base]
        return remote(base + step, send.at[step], receive.at[step], {"mp": (cp, xp, cp)[step]})

    def block_of(k):
        kx, kc = k // 2, k % 2
        return 2 * (x + kx - 2 * x * kx) + (c + kc - 2 * c * kc)

    piece_index = {name: i for i, (name, _) in enumerate(PIECES)}

    def store_piece(name, tile, value, column):
        if not dp_bits:
            target = getattr(r, "g_" + name)
            target[pl.ds(tile * 384, 384), column : column + value.shape[1]] = value
            return
        order = PIECES[piece_index[name]][1]
        weight = {bit: 1 << (len(order) - 1 - place) for place, bit in enumerate(order)}
        target = getattr(r, "b0_" + name)
        for j in range(4):
            place = (j % 2) * weight[0] + (j // 2) * weight[1] + tile * weight[2]
            target[place, :, column : column + value.shape[1]] = value[j * 96 : (j + 1) * 96].astype(BF16)

    def dp_copy(name, stage):
        order = PIECES[piece_index[name]][1]
        bit = order[stage]
        count_here = 4 >> stage
        source = getattr(r, f"b{stage}_{name}").at[pl.ds((1 - bit_of(bit)) * count_here, count_here)]
        target = getattr(r, f"x{stage}_{name}")
        return remote(DP + 3 * piece_index[name] + stage, source, target, {"dp": dp_partner(bit)})

    def dp_start(name, stage):
        if dp_bits:
            dp_copy(name, stage).start()

    def dp_finish(name, stage):
        if not dp_bits:
            return
        order = PIECES[piece_index[name]][1]
        count_here = 4 >> stage
        mine = bit_of(order[stage]) * count_here
        dp_copy(name, stage).wait_recv()
        kept = getattr(r, f"b{stage}_{name}")
        arrived = getattr(r, f"x{stage}_{name}")
        for i in range(count_here):
            total = kept[mine + i].astype(F32) + arrived[i].astype(F32)
            if stage < 2:
                getattr(r, f"b{stage + 1}_{name}")[i] = total.astype(BF16)
            else:
                getattr(r, "g_" + name)[...] = total
        if stage < 2:
            dp_copy(name, stage + 1).start()

    load(4).wait()
    ow_copy(0).start()
    ow_copy(1).start()

    for i in (0, 1, 2, 3):
        load(i).wait()
    r.wqkv[...] = jnp.concatenate([r.qw[...], r.kw[...], r.vw[...]], axis=1)
    gain_one, shift_one = row_of(r.gain_one), row_of(r.shift_one)
    q_bias, v_bias = row_of(r.q_bias), row_of(r.v_bias)
    lane = lax.broadcasted_iota(jnp.int32, (BLOCK, HD), 1)
    row_in_block = lax.broadcasted_iota(jnp.int32, (BLOCK, HD), 0)

    @pl.loop(0, blocks)
    def _(i):
        here = rows_at(i * BLOCK, BLOCK)
        std_rows, _ = standardized(r.feats[here, :].astype(F32))
        normed = (std_rows * gain_one + shift_one).astype(BF16)
        r.normed[here, :] = normed
        projected = dot(normed, r.wqkv[...])
        query = ((projected[:, :cols] + q_bias).astype(BF16).astype(F32) * SCORE_SCALE).astype(BF16)
        keys = projected[:, cols : 2 * cols].astype(BF16)
        values = (projected[:, 2 * cols :] + v_bias).astype(BF16)
        one = jnp.where(lane == 0, 1.0, 0.0).astype(BF16)
        bias = jnp.where(jnp.logical_and(lane == 0, row_in_block + i * BLOCK >= count), NEG, 0.0).astype(BF16)
        for h in range(heads):
            part = slice(h * HD, (h + 1) * HD)
            r.query[h, here, :] = jnp.concatenate([query[:, part], one], axis=1)
            r.keys[h, here, :] = jnp.concatenate([keys[:, part], bias], axis=1)
            r.values[h, here, :] = values[:, part]
        keys_t = keys.T
        values_t = values.T
        for h in range(heads):
            part = slice(h * HD, (h + 1) * HD)
            r.keys_t[h, :, here] = keys_t[part, :]
            r.values_t[h, :, here] = values_t[part, :]

    def mx_forward(h):
        mx_copy(1, h).wait_recv()
        mx_copy(2, h).start()

    @pl.loop(0, heads)
    def _(h):
        @pl.loop(0, blocks)
        def _(j):
            here = rows_at(j * BLOCK, BLOCK)
            scores = dot_nt(r.keys[h], r.query[h, here, :])
            peak = jnp.max(scores, axis=0, keepdims=True)
            exped = jnp.exp(scores - peak)
            total = jnp.sum(exped, axis=0, keepdims=True)
            mixed = dot(r.values_t[h], exped.astype(BF16)) / total
            r.mixed_t[pl.ds(pl.multiple_of(m * cols + h * HD, HD), HD), here] = mixed.astype(BF16)
            r.lse[h, :, here] = peak + jnp.log(total)

        mx_copy(0, h).start()
        mx_copy(1, h).start()

        @pl.when(h > 0)
        def _():
            mx_forward(h - 1)

    ow_copy(1).wait_recv()
    ow_copy(2).start()
    for i in (5, 6, 7):
        load(i).wait()
    slot = lax.broadcasted_iota(jnp.int32, (BLOCK, width), 0)

    @pl.loop(0, blocks)
    def _(i):
        here = rows_at(i * BLOCK, BLOCK)
        grad = r.og[here, :]
        grad = jnp.where(slot + i * BLOCK < count, grad.astype(F32), 0.0).astype(BF16)
        r.og[here, :] = grad
        r.hidden_grad[here, :] = dot_nt(grad, r.down[...])

    mx_forward(heads - 1)
    for h in range(heads):
        mx_copy(0, h).wait_recv()
        mx_copy(2, h).wait_recv()
    ow_copy(0).wait_recv()
    ow_copy(2).wait_recv()

    o_bias = row_of(r.o_bias)
    gain_two, shift_two = row_of(r.gain_two), row_of(r.shift_two)
    up_bias, down_bias = row_of(r.up_bias), row_of(r.down_bias)
    r.up_bias_sum[...] = jnp.zeros_like(r.up_bias_sum)

    @pl.loop(0, blocks)
    def _(i):
        here = rows_at(block_of(3 - i) * BLOCK, BLOCK)
        attended = dot_tn(r.mixed_t[:, here], r.ow[...])
        resid = r.feats[here, :].astype(F32) + (attended + o_bias)
        std_rows, _ = standardized(resid)
        normed_two = (std_rows * gain_two + shift_two).astype(BF16)
        r.normed_two[here, :] = normed_two
        pre_up = dot(normed_two, r.up[...]) + up_bias
        hidden, slope = gelu_pair(pre_up)
        r.hidden[here, :] = hidden.astype(BF16)
        pre_grad = (r.hidden_grad[here, :] * slope).astype(BF16)
        r.pre_grad[here, :] = pre_grad
        r.up_bias_sum[...] += column_sum(pre_grad.astype(F32))
        back = dot_nt(pre_grad, r.up[...])

        @pl.when(i == 0)
        def _():
            r.bk_tx[0] = back.astype(BF16)
            rs_copy(BK, 0).start()

        @pl.when(i == 1)
        def _():
            rs_copy(BK, 0).wait_recv()
            r.bk_tx[1] = (back + r.bk_rx[0].astype(F32)).astype(BF16)
            rs_copy(BK, 1).start()

        @pl.when(i == 2)
        def _():
            r.bk_tx[2] = back.astype(BF16)
            rs_copy(BK, 2).start()

        @pl.when(i == 3)
        def _():
            r.resid[...] = resid
            r.back[...] = back

    def grad_tiles(left, right, name, column):
        right_all = right[...]

        @pl.loop(0, 2)
        def _(t):
            value = dot_tn(left[:, rows_at(t * 384, 384)], right_all)
            store_piece(name, t, value, column)

    grad_tiles(r.og, r.hidden, "down", 0)
    dp_start("down", 0)

    own = rows_at(m * BLOCK, BLOCK)
    rs_copy(BK, 2).wait_recv()
    rs_copy(BK, 1).wait_recv()
    back = r.back[...] + r.bk_rx[2].astype(F32) + r.bk_rx[1].astype(F32)
    std_rows, inverse = standardized(r.resid[...])
    own_grad = r.og[own, :].astype(F32)
    resid_grad = own_grad + norm_back(std_rows, inverse, gain_two, back)
    resid_low = resid_grad.astype(BF16)
    r.resid_grad[...] = resid_grad
    r.resid_low[own, :] = resid_low
    rl_copy(0).start()
    rl_copy(1).start()
    r.small[2:3, :] = column_sum(resid_low.astype(F32))
    r.small[3:4, :] = column_sum(back * std_rows)
    r.small[4:5, :] = column_sum(back)
    r.small[5:6, :] = column_sum(own_grad)
    r.small[6:7, :] = r.up_bias_sum[...]

    grad_tiles(r.normed_two, r.pre_grad, "up", 0)
    dp_start("up", 0)

    @pl.loop(0, blocks)
    def _(i):
        here = rows_at(block_of(3 - i) * BLOCK, BLOCK)
        part = dot(r.hidden[here, :], r.down[...])

        @pl.when(i < 3)
        def _():
            r.ml_tx[i] = part.astype(BF16)

        @pl.when(i == 3)
        def _():
            r.ml_own[...] = part

        @pl.when(i == 0)
        def _():
            rs_copy(ML, 0).start()

        @pl.when(i == 2)
        def _():
            rs_copy(ML, 2).start()

    r.key_acc[...] = jnp.zeros_like(r.key_acc)
    r.value_acc[...] = jnp.zeros_like(r.value_acc)

    @pl.loop(0, blocks)
    def _(i):
        @pl.when(i == 1)
        def _():
            rl_copy(0).wait_recv()

        @pl.when(i == 2)
        def _():
            rl_copy(1).wait_recv()
            rl_copy(2).start()

        @pl.when(i == 3)
        def _():
            rl_copy(2).wait_recv()
            rs_copy(ML, 0).wait_recv()
            r.ml_tx[1] = (r.ml_tx[1].astype(F32) + r.ml_rx[0].astype(F32)).astype(BF16)
            rs_copy(ML, 1).start()
            dp_finish("down", 0)

        here = rows_at(block_of(i) * BLOCK, BLOCK)
        low = r.resid_low[here, :]
        ow_own = r.ow[rows_at(m * cols, 64 * 3), :]
        mixed_grad = dot_nt(low, ow_own).astype(BF16)
        mixed_grad_t = dot_nt(ow_own, low).astype(BF16).astype(F32)
        inner = mixed_grad_t * r.mixed_t[rows_at(m * cols, 64 * 3), here].astype(F32)
        for h in range(heads):
            r.mixed_grad[h] = mixed_grad[:, h * HD : (h + 1) * HD]
            r.inner[h] = column_sum(inner[h * HD : (h + 1) * HD])

        @pl.loop(0, heads)
        def _(h):
            query = r.query[h, here, :]
            grad = r.mixed_grad[h]
            scores = dot_nt(r.keys[h], query)
            probs = jnp.exp(scores - r.lse[h, :, here])
            prob_grad = dot_nt(r.values[h], grad)
            score_grad = (probs * (prob_grad - r.inner[h])).astype(BF16)
            r.value_acc[h] += dot(probs.astype(BF16), grad)
            r.key_acc[h] += dot(score_grad, query)
            query_grad = dot(r.keys_t[h], score_grad) * SCORE_SCALE
            r.query_grad[h, here, :] = query_grad.T.astype(BF16)

    dp_finish("up", 0)

    @pl.loop(0, blocks)
    def _(i):
        here = rows_at(i * BLOCK, BLOCK)
        parts = [r.query_grad[h, here, :] for h in range(heads)]
        parts += [r.key_acc[h, here, :][:, :HD].astype(BF16) for h in range(heads)]
        parts += [r.value_acc[h, here, :].astype(BF16) for h in range(heads)]
        r.dqkv[here, :] = jnp.concatenate(parts, axis=1)

    @pl.loop(0, 2)
    def _(t):
        columns = rows_at(t * 384, 384)
        value = dot_tn(r.normed[:, columns], r.dqkv[...])
        store_piece("qk", t, value[:, : 2 * cols], 0)
        store_piece("vo", t, value[:, 2 * cols :], 0)
        out_grad_t = dot(r.mixed_t[rows_at(m * cols, 64 * 3), :], r.resid_low[:, columns])
        store_piece("vo", t, out_grad_t.T, cols)

    dp_start("qk", 0)
    dp_start("vo", 0)
    dp_finish("down", 1)

    r.gain_sum[...] = jnp.zeros_like(r.gain_sum)
    r.shift_sum[...] = jnp.zeros_like(r.shift_sum)
    r.bias_sum[...] = jnp.zeros_like(r.bias_sum)

    @pl.loop(0, blocks)
    def _(i):
        here = rows_at(block_of(3 - i) * BLOCK, BLOCK)
        part_grads = r.dqkv[here, :]
        part = dot_nt(part_grads, r.wqkv[...])

        @pl.when(i == 0)
        def _():
            r.in_tx[0] = part.astype(BF16)
            rs_copy(IN, 0).start()

        @pl.when(i == 1)
        def _():
            rs_copy(IN, 0).wait_recv()
            r.in_tx[1] = (part + r.in_rx[0].astype(F32)).astype(BF16)
            rs_copy(IN, 1).start()

        @pl.when(i == 2)
        def _():
            r.in_tx[2] = part.astype(BF16)
            rs_copy(IN, 2).start()

        @pl.when(i == 3)
        def _():
            r.back[...] = part

        std_rows, _ = standardized(r.feats[here, :].astype(F32))
        r.gain_sum[...] += column_sum(part * std_rows)
        r.shift_sum[...] += column_sum(part)
        r.bias_sum[...] += column_sum(part_grads.astype(F32))

    r.small[0:1, :] = r.gain_sum[...]
    r.small[1:2, :] = r.shift_sum[...]
    r.small[7:8, :] = jnp.concatenate([r.bias_sum[...], jnp.zeros((1, width - 3 * cols), F32)], axis=1)

    sm_partners = [{"dp": dp_partner(bit)} for bit in range(dp_bits)] + [{"mp": cp}, {"mp": xp}]

    def sm_copy(stage):
        source = r.small if stage == 0 else r.sm_sum.at[stage - 1]
        return remote(SM + stage, source, r.sm_rx.at[stage], sm_partners[stage])

    def sm_finish(stage):
        sm_copy(stage).wait_recv()
        kept = r.small[...] if stage == 0 else r.sm_sum[stage - 1]
        arrived = r.sm_rx[stage]
        if stage >= dp_bits:
            arrived = jnp.where(lax.broadcasted_iota(jnp.int32, arrived.shape, 0) < 6, arrived, 0.0)
        total = kept + arrived
        if stage < len(sm_partners) - 1:
            r.sm_sum[stage] = total
            sm_copy(stage + 1).start()
        else:
            r.small_out[...] = total

    sm_copy(0).start()
    dp_finish("up", 1)
    rs_copy(ML, 1).wait_recv()
    rs_copy(ML, 2).wait_recv()
    mlp = r.ml_own[...] + r.ml_rx[2].astype(F32) + r.ml_rx[1].astype(F32)
    r.layer_out[...] = (r.resid[...] + (mlp + down_bias)).astype(BF16)
    sm_finish(0)
    dp_finish("qk", 0)
    dp_finish("vo", 0)
    sm_finish(1)
    rs_copy(IN, 2).wait_recv()
    rs_copy(IN, 1).wait_recv()
    back = r.back[...] + r.in_rx[2].astype(F32) + r.in_rx[1].astype(F32)
    std_rows, inverse = standardized(r.feats[own, :].astype(F32))
    r.feats_grad[...] = (r.resid_grad[...] + norm_back(std_rows, inverse, gain_one, back)).astype(BF16)
    for stage in range(2, len(sm_partners)):
        sm_finish(stage)
    dp_finish("qk", 1)
    dp_finish("vo", 1)
    for name, _ in PIECES:
        dp_finish(name, 2)

    for kind in range(3):
        ow_copy(kind).wait_send()
        rl_copy(kind).wait_send()
        for h in range(heads):
            mx_copy(kind, h).wait_send()
        for base in (BK, ML, IN):
            rs_copy(base, kind).wait_send()
    for stage in range(len(sm_partners)):
        sm_copy(stage).wait_send()
    if dp_bits:
        for name, _ in PIECES:
            for stage in range(3):
                dp_copy(name, stage).wait_send()


PIECE_COLUMNS = {"down": 768, "up": 768, "qk": 384, "vo": 384}


def layer_call(dp_size, clip_feats, counts, gain_one, shift_one, q_weight, k_weight, v_weight, q_bias, v_bias, o_weight,
               o_bias, gain_two, shift_two, up_weight, up_bias, down_weight, down_bias, out_grad):
    rows, width = clip_feats.shape
    cols = q_weight.shape[1]
    heads = cols // HD
    hidden_cols = up_weight.shape[1]
    dp_bits = 3 if dp_size == 8 else 0
    vmem = pl.BlockSpec(memory_space=pltpu.VMEM)
    anywhere = pl.BlockSpec(memory_space=pl.ANY)
    inputs = {
        "counts": (counts, pl.BlockSpec(memory_space=pltpu.SMEM)),
        "gain_one": (gain_one, vmem), "shift_one": (shift_one, vmem), "q_bias": (q_bias, vmem), "v_bias": (v_bias, vmem),
        "o_bias": (o_bias, vmem), "gain_two": (gain_two, vmem), "shift_two": (shift_two, vmem), "up_bias": (up_bias, vmem),
        "down_bias": (down_bias, vmem),
        "feats_hbm": (clip_feats, anywhere), "qw_hbm": (q_weight, anywhere), "kw_hbm": (k_weight, anywhere),
        "vw_hbm": (v_weight, anywhere), "ow_hbm": (o_weight, anywhere), "up_hbm": (up_weight, anywhere),
        "down_hbm": (down_weight, anywhere), "og_hbm": (out_grad, anywhere),
    }
    shard = width // dp_size if dp_bits else width
    outputs = {"layer_out": ((BLOCK, width), BF16), "feats_grad": ((BLOCK, width), BF16), "small_out": ((8, width), F32)}
    for name, _ in PIECES:
        outputs["g_" + name] = ((shard, PIECE_COLUMNS[name]), F32)
    piece = (BLOCK, width)
    scratch = {
        "feats": ((rows, width), BF16), "qw": ((width, cols), BF16), "kw": ((width, cols), BF16), "vw": ((width, cols), BF16),
        "wqkv": ((width, 3 * cols), BF16), "ow": ((width, width), BF16), "og": ((rows, width), BF16),
        "down": ((hidden_cols, width), BF16), "up": ((width, hidden_cols), BF16), "normed": ((rows, width), BF16),
        "query": ((heads, rows, 2 * HD), BF16), "keys": ((heads, rows, 2 * HD), BF16), "values": ((heads, rows, HD), BF16),
        "keys_t": ((heads, HD, rows), BF16), "values_t": ((heads, HD, rows), BF16), "mixed_t": ((width, rows), BF16),
        "lse": ((heads, 1, rows), F32), "hidden_grad": ((rows, hidden_cols), F32), "resid": (piece, F32),
        "normed_two": ((rows, width), BF16), "hidden": ((rows, hidden_cols), BF16), "pre_grad": ((rows, hidden_cols), BF16),
        "up_bias_sum": ((1, hidden_cols), F32), "back": (piece, F32), "resid_grad": (piece, F32),
        "resid_low": ((rows, width), BF16), "ml_own": (piece, F32),
        "bk_tx": ((3,) + piece, BF16), "bk_rx": ((3,) + piece, BF16), "ml_tx": ((3,) + piece, BF16),
        "ml_rx": ((3,) + piece, BF16), "in_tx": ((3,) + piece, BF16), "in_rx": ((3,) + piece, BF16),
        "mixed_grad": ((heads, BLOCK, HD), BF16), "inner": ((heads, 1, BLOCK), F32),
        "key_acc": ((heads, rows, 2 * HD), F32), "value_acc": ((heads, rows, HD), F32),
        "query_grad": ((heads, rows, HD), BF16), "dqkv": ((rows, 3 * cols), BF16),
        "gain_sum": ((1, width), F32), "shift_sum": ((1, width), F32), "bias_sum": ((1, 3 * cols), F32),
        "small": ((8, width), F32), "sm_sum": ((dp_bits + 1, 8, width), F32), "sm_rx": ((dp_bits + 2, 8, width), F32),
    }
    if dp_bits:
        for name, _ in PIECES:
            for stage in range(3):
                scratch[f"b{stage}_{name}"] = ((8 >> stage, shard, PIECE_COLUMNS[name]), BF16)
                scratch[f"x{stage}_{name}"] = ((4 >> stage, shard, PIECE_COLUMNS[name]), BF16)
    copies = 24 + dp_bits + 2 + 12
    names = list(inputs) + list(outputs) + list(scratch) + ["load_sem", "send_sem", "recv_sem"]
    results = pl.pallas_call(
        functools.partial(layer_kernel, names, dp_bits),
        out_shape=[jax.ShapeDtypeStruct(*spec) for spec in outputs.values()],
        in_specs=[spec for _, spec in inputs.values()],
        out_specs=[vmem] * len(outputs),
        scratch_shapes=[pltpu.VMEM(*spec) for spec in scratch.values()]
        + [pltpu.SemaphoreType.DMA((8,)), pltpu.SemaphoreType.DMA((copies,)), pltpu.SemaphoreType.DMA((copies,))],
        compiler_params=pltpu.CompilerParams(collective_id=0, has_side_effects=True, vmem_limit_bytes=67043328),
        name="layer",
    )(*[value for value, _ in inputs.values()])
    return dict(zip(outputs, results))


def shards(dp_size, *args):
    out = layer_call(dp_size, *args)
    cols = args[4].shape[1]
    small = out["small_out"]
    width = small.shape[1]
    d, m = lax.axis_index("dp"), lax.axis_index("mp")

    def over(value, dim):
        return value if dp_size == 8 else lax.psum_scatter(value, "dp", scatter_dimension=dim, tiled=True)

    if dp_size != 8:
        small = lax.psum(small, "dp")
    g_qk, g_vo = out["g_qk"], out["g_vo"]
    piece = width // (dp_size * 4)
    group = [lax.dynamic_slice(small, (i, (d * 4 + m) * piece), (1, piece)).reshape(piece) for i in range(6)]
    up_piece = args[14].shape[0] // dp_size
    head_piece = cols // dp_size
    up_bias = lax.dynamic_slice(small, (6, d * up_piece), (1, up_piece)).reshape(up_piece)
    q_bias = lax.dynamic_slice(small, (7, d * head_piece), (1, head_piece)).reshape(head_piece)
    v_bias = lax.dynamic_slice(small, (7, 2 * cols + d * head_piece), (1, head_piece)).reshape(head_piece)
    return (
        out["layer_out"], out["feats_grad"], group[0], group[1],
        over(g_qk[:, :cols], 0), over(g_qk[:, cols:], 0), over(g_vo[:, :cols], 0), q_bias, v_bias,
        over(g_vo[:, cols:].T, 1), group[2], group[3], group[4], over(out["g_up"], 0), up_bias, over(out["g_down"].T, 1),
        group[5],
    )


def solution(mesh):
    placed = (
        P("dp", None), P("dp"), P(), P(), P(None, "mp"), P(None, "mp"), P(None, "mp"), P("mp"), P("mp"), P("mp", None),
        P(), P(), P(), P(None, "mp"), P("mp"), P("mp", None), P(), P("dp", None),
    )
    return jax.shard_map(
        functools.partial(shards, mesh.shape["dp"]),
        mesh=mesh,
        in_specs=placed,
        out_specs=(
            P(("dp", "mp"), None), P(("dp", "mp"), None), P(("dp", "mp")), P(("dp", "mp")), P("dp", "mp"), P("dp", "mp"),
            P("dp", "mp"), P(("mp", "dp")), P(("mp", "dp")), P("mp", "dp"), P(("dp", "mp")), P(("dp", "mp")),
            P(("dp", "mp")), P("dp", "mp"), P(("mp", "dp")), P("mp", "dp"), P(("dp", "mp")),
        ),
        check_vma=False,
    )
```

time: 637 us -> 109 us (0.17)
  waiting for transfers between devices: 408 us -> 0 us
  Pallas kernels: 0 us -> 92.8 us
  matrix products: 73.9 us -> 0 us
  blocking collectives: 61.5 us -> 0 us
  other arithmetic: 52.5 us -> 0 us
  between operations: 16.8 us -> 1.39 us
  local copies, waits for them, and re-layouts: 22.1 us -> 14.1 us
    reduce_scatter x7 -> x0, waiting for transfers between devices: 325 us -> none  [the longest x1 72.8 us: shards(): lax.psum_scatter(up_weight_grad, 'dp', scatter_dimension=0, tiled=True)]
    pallas_call x0 -> x1, Pallas kernels: none -> 92.8 us  [layer_call(): pl.pallas_call(functools.partial(layer_kernel, names, dp_bits), out_shape...]
    psum x2 -> x0, waiting for transfers between devices: 82.2 us -> none  [the longest x1 43 us: shards(): lax.psum(product_nt(pre_grad, up_weight).astype(jnp.bfloat16), 'mp')]
    dot_general x31 -> x0, matrix products: 72.3 us -> none  [the longest x6 22.1 us: product(): return jnp.dot(left, right, preferred_element_type=jnp.float32)]
    unnamed x2 -> x0, blocking collectives: 61.5 us -> none
    reduce_sum x17 -> x0, other arithmetic: 26.9 us -> none  [the longest x5 9.15 us: standardize(): centered = values - jnp.mean(values, axis=-1, keepdims=True)]
    convert_element_type x17 -> x0, other arithmetic: 22.4 us -> none  [the longest x1 3.48 us: shards(): resid_low = resid_grad.astype(jnp.bfloat16)]
    unnamed x102 -> x16, local copies, waits for them, and re-layouts: 14.7 us -> 9.38 us
  transfers between devices with their start and end apart: 10 -> 0, of which waited for: 9 -> 0; matrix products, arithmetic and copies ran while one was open for 13% -> 0% of each run, Pallas kernels for 0% -> 0%
where the time goes in v1:
time: 109 us; the launch traced here: 108 us
  Pallas kernels  92.8 us (85%)
  local copies, waits for them, and re-layouts  14.1 us (13%)
  between operations  1.39 us (1%)
    pallas_call x1, Pallas kernels, layer_call(): pl.pallas_call(functools.partial(layer_kernel, names, dp_bits), out_shape...  92.8 us
    unnamed x16, local copies, waits for them, and re-layouts  9.38 us

profile of v1, /device:TPU:0, one launch (start us, length us, event | category | flops | bytes accessed | tf_op | source)
XLA Modules:
  0.0 108.3 jit_solution(2202983196710508279)
XLA Ops:
  0.7 0.0 copy-start.3
  1.4 1.9 %copy.35.refs_11_ = bf16[768,192]{1,0:T(8,128)(2,1)} copy(bf16[768,192]{0,1:T(8,128)(2,1)} %param.22) | data formatting | bytes 589824 | tf_op args[4]
  3.2 1.9 %copy.36.refs_12_ = bf16[768,192]{1,0:T(8,128)(2,1)} copy(bf16[768,192]{0,1:T(8,128)(2,1)} %param.23) | data formatting | bytes 589824 | tf_op args[5]
  5.1 0.0 copy-done.3
  5.1 0.9 copy.37.refs_13_
  6.0 92.8 %layer.1 = (bf16[256,768]{1,0:T(8,128)(2,1)}, bf16[256,768]{1,0:T(8,128)(2,1)}, f32[8,768]{1,0:T(8,128)}, f32[96,768]{1,0:T(8,128)}, f32[96,768]{1,0:T(8,128)}, /*index=5*/f32[96,384]{1,0:T(8,128)}, f32[96,384]{1,0:T(8,128)}) custom-call(s32[1]{0:T(128)S(6)} %copy.43.refs_0_, bf16[768]{0:T(1024)(128)(2,1)} %refs_1_.1, bf16[768]{0:T(1024)(128)(2,1)} %refs_2_.1, ...), custom_call_target="tpu_custom_call" | custom-call | tf_op jit(solution)/shard_map/layer/pallas_call | solution.py:575
  98.9 0.0 copy-start
  98.9 0.0 copy-start.2
  98.9 1.6 %dynamic-slice_bitcast_fusion = (f32[24]{0:T(128)}, f32[24]{0:T(128)}, f32[24]{0:T(128)}, f32[24]{0:T(128)}, f32[24]{0:T(128)}, /*index=5*/f32[24]{0:T(128)}, f32[24]{0:T(128)}, f32[24]{0:T(128)}) fusion(f32[8,768]{1,0:T(8,128)} %get-tuple-element.26, s32[]{:T(128)S(6)} %select_n.8, s32[]{:T(128)S(6)} %select_n.19, s32[]{:T(128)S(6)} %select_n.18), kind=kLoop, calls=%fused_computation.5 | loop fusion | bytes 1548 | tf_op jit(solution)/shard_map/reshape | solution.py:602
  100.5 0.0 copy-start.1
  100.5 1.8 %slice_bitcast_fusion = (f32[192,96]{0,1:T(8,128)S(1)}, f32[96,192]{1,0:T(8,128)}, f32[96,192]{1,0:T(8,128)}, f32[96,192]{1,0:T(8,128)}) fusion(f32[96,384]{1,0:T(8,128)} %get-tuple-element.28, f32[96,384]{1,0:T(8,128)} %get-tuple-element.27), kind=kLoop, calls=%fused_computation | loop fusion | bytes 589824 | tf_op jit(solution)/shard_map/transpose | solution.py:611
  102.3 0.7 copy.38
  103.1 1.3 %dynamic-slice_bitcast_fusion.1 = f32[96]{0:T(128)} fusion(f32[8,768]{1,0:T(8,128)} %get-tuple-element.26, s32[]{:T(128)S(6)} %select_n.20), kind=kLoop, calls=%fused_computation.6 | loop fusion | bytes 772 | tf_op jit(solution)/shard_map/reshape | solution.py:605
  104.4 1.8 %copy.44 = bf16[256,768]{1,0:T(8,128)(2,1)} copy(bf16[256,768]{1,0:T(8,128)(2,1)} %get-tuple-element.79) | data formatting | bytes 786432
  106.1 0.0 copy-done
  106.1 0.7 copy.45
  106.9 0.0 copy-done.2
  106.9 0.7 copy.46
  107.6 0.0 copy-done.1
  107.6 0.7 copy.47
Async XLA Ops:
  0.7 4.5 %copy-start.3 = (bf16[768,192]{0,1:T(8,128)(2,1)S(1)}, bf16[768,192]{0,1:T(8,128)(2,1)}, u32[]{:S(2)}) copy-start(bf16[768,192]{0,1:T(8,128)(2,1)} %param.24) | copy-start | bytes 884740
  98.9 7.2 %copy-start = (bf16[256,768]{1,0:T(8,128)(2,1)S(1)}, bf16[256,768]{1,0:T(8,128)(2,1)}, u32[]{:S(2)}) copy-start(bf16[256,768]{1,0:T(8,128)(2,1)} %get-tuple-element.80) | copy-start | bytes 1179652
  98.9 8.0 %copy-start.2 = (f32[96,768]{1,0:T(8,128)S(1)}, f32[96,768]{1,0:T(8,128)}, u32[]{:S(2)}) copy-start(f32[96,768]{1,0:T(8,128)} %get-tuple-element.92) | copy-start | bytes 884740
  100.5 7.1 %copy-start.1 = (f32[96,768]{1,0:T(8,128)S(1)}, f32[96,768]{1,0:T(8,128)}, u32[]{:S(2)}) copy-start(f32[96,768]{1,0:T(8,128)} %get-tuple-element.30) | copy-start | bytes 884740

commit v2 on v1

v2 whole, which is shorter than its diff:
```python
import functools
import types

import jax
import jax.numpy as jnp
from jax import lax
from jax.experimental import pallas as pl
from jax.experimental.pallas import tpu as pltpu
from jax.sharding import PartitionSpec as P

HD = 64
NORM_EPSILON = 1e-06
SCORE_SCALE = 0.125
BLOCK = 256
MESH = pl.DeviceIdType.MESH
F32 = jnp.float32
BF16 = jnp.bfloat16
DP, MP = "dp", "mp"
INV_SQRT2 = 0.7071067811865476
INV_SQRT_2PI = 0.3989422804014327
NEG = -1e30

YN, NY, YD, ZYZ, YZZ = range(5)
HALVED = {ZYZ: (1, 0, 2), YZZ: (0, 1, 2)}
DOWN0, DOWN1, UP0, UP1, HEAD0, HEAD1, HEAD2, OUT = range(8)
PLANS = (YN, NY, YN, YN, YZZ, YZZ, YZZ, YZZ)
COLUMNS = (384, 384, 384, 384, 192, 192, 192, 192)
HELD = {YN: (8, 4, 2), NY: (8, 4, 2), YD: (8, 4), ZYZ: (8, 4, 2), YZZ: (8, 4, 2)}
ARRIVING = {YN: (4, 2, 2, 1), NY: (4, 4, 2, 1), YD: (4, 3), ZYZ: (4, 2, 1), YZZ: (4, 2, 1)}


POLLS = (
    ((DOWN0, 0), (DOWN1, 0)),
    (),
    (),
    ((UP0, 0), (DOWN0, 1)),
    ((DOWN1, 1),),
    (),
    ((UP1, 0), (DOWN0, 2)),
    ((UP0, 1),),
    ((DOWN1, 2), (UP1, 1), (HEAD0, 0)),
    ((UP0, 2), (DOWN0, 3), (HEAD1, 0), (UP1, 2), (HEAD2, 0), (OUT, 0)),
    ((UP0, 3), (DOWN1, 3), (HEAD0, 1), (HEAD1, 1), (HEAD2, 1), (OUT, 1), (UP1, 3)),
    ((HEAD0, 2), (HEAD1, 2), (HEAD2, 2), (OUT, 2)),
)


def packed_shape(piece, rows):
    columns = COLUMNS[piece]
    return (rows, columns) if columns == 384 else (rows // 2, 2 * columns)


def dot(left, right):
    return jnp.dot(left, right, preferred_element_type=F32)


def dot_nt(left, right):
    return lax.dot_general(left, right, (((1,), (1,)), ((), ())), preferred_element_type=F32)


def dot_tn(left, right):
    return lax.dot_general(left, right, (((0,), (0,)), ((), ())), preferred_element_type=F32)


def standardized(values):
    centered = values - jnp.mean(values, axis=-1, keepdims=True)
    variance = jnp.mean(centered * centered, axis=-1, keepdims=True)
    inverse = lax.rsqrt(variance + NORM_EPSILON)
    return centered * inverse, inverse


def norm_back(std_rows, inverse, gain, grad):
    scaled = gain * grad
    mean_scaled = jnp.mean(scaled, axis=-1, keepdims=True)
    mean_inner = jnp.mean(scaled * std_rows, axis=-1, keepdims=True)
    return inverse * (scaled - mean_scaled - std_rows * mean_inner)


def gelu_pair(values):
    bell = jnp.exp(-0.5 * (values * values))
    t = 1.0 / (1.0 + (0.3275911 * INV_SQRT2) * jnp.abs(values))
    tail = t * (0.127414796 + t * (-0.142248368 + t * (0.7107068705 + t * (-0.7265760135 + t * 0.5307027145)))) * bell
    phi = jnp.where(values >= 0.0, 1.0 - tail, tail)
    return values * phi, phi + values * (bell * INV_SQRT_2PI)


def column_sum(values):
    return jnp.sum(values, axis=0, keepdims=True)


def row_of(ref):
    return ref[...].astype(F32).reshape(1, -1)


def layer_kernel(names, dp_bits, *refs):
    r = types.SimpleNamespace(**dict(zip(names, refs)))
    of_pieces = iter(refs[len(names) :])
    grad_outs = [next(of_pieces) for _ in PLANS]
    grads = [next(of_pieces) for _ in PLANS]
    held = [[next(of_pieces) for _ in HELD[plan]] for plan in PLANS] if dp_bits else []
    arrived = [[next(of_pieces) for _ in ARRIVING[plan]] for plan in PLANS] if dp_bits else []
    rows, width = r.feats_hbm.shape
    heads = r.qw_hbm.shape[0]
    cols = heads * HD
    blocks = rows // BLOCK

    m = lax.axis_index(MP)
    c = m % 2
    x = m // 2
    cp = m + 1 - 2 * c
    xp = m + 2 - 4 * x

    def bit_of(bit):
        return (lax.axis_index(DP) // (1 << bit)) % 2

    def dp_peer(mask):
        peer = lax.axis_index(DP)
        for bit in range(3):
            if mask >> bit & 1:
                peer = peer + (1 << bit) * (1 - 2 * bit_of(bit))
        return peer

    def block_of(k):
        kx, kc = k // 2, k % 2
        return 2 * (x + kx - 2 * x * kx) + (c + kc - 2 * c * kc)

    def rows_at(start, size):
        return pl.ds(pl.multiple_of(start, size), size)

    own_heads = pl.ds(pl.multiple_of(m * cols, 64), cols)
    own = rows_at(m * BLOCK, BLOCK)

    first = dict(
        counts=(r.counts_hbm, r.counts), ow=(r.ow_hbm, r.ow.at[own_heads, :]), qw=(r.qw_hbm, r.wqkv.at[:, pl.ds(0, HD), :]),
        kw=(r.kw_hbm, r.wqkv.at[:, pl.ds(HD, HD), :]), vw=(r.vw_hbm, r.wqkv.at[:, pl.ds(2 * HD, HD), :]),
        gain_one=(r.gain_one_hbm, r.gain_one), shift_one=(r.shift_one_hbm, r.shift_one), q_bias=(r.q_bias_hbm, r.q_bias),
        v_bias=(r.v_bias_hbm, r.v_bias),
    )
    second = dict(
        o_bias=(r.o_bias_hbm, r.o_bias), gain_two=(r.gain_two_hbm, r.gain_two), shift_two=(r.shift_two_hbm, r.shift_two),
        up_bias=(r.up_bias_hbm, r.up_bias), down_bias=(r.down_bias_hbm, r.down_bias), og=(r.og_hbm, r.og),
        down=(r.down_hbm, r.down), up=(r.up_hbm, r.up),
    )
    loads = {**first, **second}
    load_index = {name: i for i, name in enumerate(loads)}

    def load(name):
        return pltpu.make_async_copy(*loads[name], r.load_sem.at[load_index[name]])

    def load_feats(i):
        here = rows_at(i * BLOCK, BLOCK)
        return pltpu.make_async_copy(r.feats_hbm.at[here, :], r.feats.at[here, :], r.load_sem.at[len(loads) + i])

    for name in first:
        load(name).start()
    for i in range(blocks):
        load_feats(i).start()
    for name in second:
        load(name).start()

    barrier = pltpu.get_barrier_semaphore()
    mp_peers = {1: cp, 2: xp, 3: block_of(3)}
    partners = [{MP: peer} for peer in mp_peers.values()] + [{DP: dp_peer(k)} for k in range(1, 1 << dp_bits)]
    for partner in partners:
        pl.semaphore_signal(barrier, inc=1, device_id=partner, device_id_type=MESH)

    def remote(index, source, target, partner):
        return pltpu.make_async_remote_copy(
            src_ref=source, dst_ref=target, send_sem=r.send_sem.at[index], recv_sem=r.recv_sem.at[index],
            device_id=partner, device_id_type=MESH,
        )

    OW, RL, BK, ML, IN, MG, SG, SD, MX = 0, 3, 6, 9, 13, 16, 19, 22, 29
    PIECE = MX + 12

    def ow_copy(kind):
        view = r.ow.at[pl.ds(pl.multiple_of((m, m, xp)[kind] * cols, 64), cols), :]
        return remote(OW + kind, view, view, {MP: (cp, xp, cp)[kind]})

    def mx_copy(kind, turn, place):
        owner = (m, m, xp)[kind]
        block = block_of(2 * turn + place if kind < 2 else 2 * (1 - turn) + place)
        view = r.mixed_t.at[block, pl.ds(pl.multiple_of(owner * cols, 64), cols), :]
        return remote(MX + (kind * 2 + turn) * 2 + place, view, view, {MP: (cp, xp, cp)[kind]})

    def rl_copy():
        return remote(RL, r.resid_low.at[c], r.resid_low.at[c], {MP: cp})

    def go_copy():
        return remote(RL + 1, r.go_tx, r.go_rx, {MP: xp})

    def rs_copy(base, step):
        send, receive = {BK: (r.bk_tx, r.bk_rx), ML: (r.ml_tx, r.ml_rx), IN: (r.bk_tx, r.in_rx)}[base]
        return remote(base + step, send.at[step], receive.at[step], {MP: (cp, xp, cp)[step]})

    def ml_x_copy(half):
        part = pl.ds(half * (BLOCK // 2), BLOCK // 2)
        return remote((ML + 1, ML + 3)[half], r.ml_tx.at[1, part], r.ml_rx.at[1, part], {MP: xp})

    def mg_copy(k):
        return remote(MG + k - 1, r.mg_tx.at[k - 1], r.mixed_grad_t.at[m], {MP: mp_peers[k]})

    def sg_copy(k):
        return remote(SG + k - 1, r.small_dp, r.sg_rx.at[k - 1], {MP: mp_peers[k]})

    def sd_copy(k):
        return remote(SD + k - 1, r.small_tx.at[dp_peer(k)], r.sd_rx.at[k - 1], {DP: dp_peer(k)})

    def store_piece(piece, tile, value):
        if not dp_bits:
            grads[piece][pl.ds(tile * 384, 384), :] = value
            return
        columns = COLUMNS[piece]
        weight = {YN: (4, 1, 2), YD: (4, 1, 2), NY: (1, 2, 4), ZYZ: (2, 4, 1), YZZ: (4, 2, 1)}[PLANS[piece]]
        for j in range(4):
            place = (j % 2) * weight[0] + (j // 2) * weight[1] + tile * weight[2]
            block = value[j * 96 : (j + 1) * 96].astype(BF16)
            if columns == 384:
                held[piece][0][place] = block
            else:
                held[piece][0][place, :, :columns] = block[:48]
                held[piece][0][place, :, columns:] = block[48:]

    y, z = bit_of(0), lax.axis_index(DP) // 2
    side, inner = z // 2, ((z + 1) // 2) % 2
    facing = side + inner - 2 * side * inner

    def part(ref, start, count):
        return ref.at[pl.ds(start, count)]

    def dp_remote(piece, stage, source, mask, target=None):
        target = arrived[piece][stage] if target is None else target
        return remote(PIECE + 4 * piece + stage, source, target, {DP: dp_peer(mask)})

    def dp_copies(piece, stage):
        plan, mine = PLANS[piece], held[piece]
        if plan in HALVED:
            bit = HALVED[plan][stage]
            count = 4 >> stage
            return [(None, lambda: dp_remote(piece, stage, part(mine[stage], (1 - bit_of(bit)) * count, count), 1 << bit))]
        if plan == YD and stage == 1:
            return [
                (None, lambda k=k: remote(PIECE + 4 * piece + k, mine[1].at[dp_peer(2 * k) // 2], arrived[piece][1].at[k - 1],
                                          {DP: dp_peer(2 * k)}))
                for k in (3, 2, 1)
            ]
        if stage == (3 if plan == NY else 0):
            count = 1 if plan == NY else 4
            source = mine[2] if plan == NY else mine[0]
            return [(None, lambda: dp_remote(piece, stage, part(source, (1 - y) * count, count), 1))]
        size = 2 if plan == NY else 1
        step = stage if plan == NY else stage - 1
        pair = mine[1 if plan == NY else 2]
        if step == 0:
            return [(None, lambda: dp_remote(piece, stage, part(mine[0 if plan == NY else 1], 2 * size * (1 - facing), 2 * size), 2))]
        if step == 1:
            return [(1, lambda: dp_remote(piece, stage, pair, 6))]
        place = (1 - z % 2) * size
        return [
            (1, lambda: dp_remote(piece, stage, part(arrived[piece][stage - 1], place, size), 2)),
            (0, lambda: dp_remote(piece, stage, part(pair, place, size), 2)),
        ]

    def each(piece, stage, action, only=None):
        for flag, make in dp_copies(piece, stage):
            if flag is None:
                action(make())
            elif only is None or only == flag:

                @pl.when(inner == flag)
                def _():
                    action(make())

    def start(copy):
        copy.start()

    def arrive(copy):
        copy.wait_recv()

    def leave(copy):
        copy.wait_send()

    def dp_start(*pieces):
        if dp_bits:
            for piece in pieces:
                each(piece, 0, start)

    def summed(first_ref, first_place, second_ref, second_place, count, target):
        for i in range(count):
            total = first_ref[first_place + i].astype(F32) + second_ref[second_place + i].astype(F32)
            if target is None:
                return total
            target[i] = total.astype(BF16)

    def dp_finish(stage, *pieces):
        for piece in pieces if dp_bits else ():
            plan, mine, came = PLANS[piece], held[piece], arrived[piece]
            if plan in HALVED:
                each(piece, stage, arrive)
                count = 4 >> stage
                kept = bit_of(HALVED[plan][stage]) * count
                if stage < 2:
                    summed(mine[stage], kept, came[stage], 0, count, mine[stage + 1])
                    each(piece, stage + 1, start)
                else:
                    grads[piece][...] = summed(mine[2], kept, came[2], 0, 1, None)
                continue
            if plan == YD and stage == 1:
                total = mine[1][z].astype(F32)
                each(piece, 1, arrive)
                for k in range(3):
                    total = total + came[1][k].astype(F32)
                grads[piece][...] = total
                continue
            if plan != NY and stage == 0:
                each(piece, 0, arrive)
                summed(mine[0], 4 * y, came[0], 0, 4, mine[1])
                each(piece, 1, start)
                continue
            if plan == NY and stage == 3:
                each(piece, 3, arrive)
                grads[piece][...] = summed(mine[2], y, came[3], 0, 1, None)
                continue
            size = 2 if plan == NY else 1
            step = stage if plan == NY else stage - 1
            pair = mine[1 if plan == NY else 2]
            if step == 0:
                each(piece, stage, arrive)
                summed(mine[0 if plan == NY else 1], 2 * size * facing, came[stage], 0, 2 * size, pair)
                each(piece, stage + 1, start, 1)
                each(piece, stage + 2, start, 0)
            elif step == 1:
                each(piece, stage, arrive, 1)
                each(piece, stage + 1, start, 1)
            else:
                arrive(dp_copies(piece, stage)[0][1]())
                place = (z % 2) * size
                for flag, source in ((1, came[stage - 1]), (0, pair)):

                    @pl.when(inner == flag)
                    def _():
                        if plan == NY:
                            summed(source, place, came[stage], 0, 2, mine[2])
                        else:
                            grads[piece][...] = summed(source, place, came[stage], 0, 1, None)

                if plan == NY:
                    each(piece, stage + 1, start)

    done = [(r.layer_out_v, r.layer_out), (r.feats_grad_v, r.feats_grad), (r.small_out_v, r.small_out)]
    done += list(zip(grads, grad_outs))

    def write_out(i):
        return pltpu.make_async_copy(*done[i], r.out_sem.at[i])

    def poll(point):
        for piece, stage in POLLS[point] if dp_bits else ():
            dp_finish(stage, piece)
            if stage == len(ARRIVING[PLANS[piece]]) - 1:
                write_out(3 + piece).start()

    pl.semaphore_wait(barrier, len(partners))
    load("ow").wait()
    ow_copy(1).start()
    ow_copy(0).start()
    for name in first:
        if name != "ow":
            load(name).wait()
    count = r.counts[0]
    gain_one, shift_one = row_of(r.gain_one), row_of(r.shift_one)
    q_bias = jnp.broadcast_to(row_of(r.q_bias), (128, cols)).T[:, :1]
    v_bias = jnp.broadcast_to(row_of(r.v_bias), (128, cols)).T[:, :1]
    lane = lax.broadcasted_iota(jnp.int32, (HD, BLOCK), 1)
    first_row = lax.broadcasted_iota(jnp.int32, (HD, BLOCK), 0) == 0
    one = jnp.where(first_row, 1.0, 0.0).astype(BF16)

    @pl.loop(0, blocks)
    def _(i):
        here = rows_at(i * BLOCK, BLOCK)
        load_feats(i).wait()
        std_rows, _ = standardized(r.feats[here, :].astype(F32))
        r.std_one[here, :] = std_rows.astype(BF16)
        normed = (std_rows * gain_one + shift_one).astype(BF16)
        r.normed[here, :] = normed
        projected = dot_nt(r.wqkv[...].reshape(3 * cols, width), normed)
        bias = jnp.where(jnp.logical_and(first_row, lane + i * BLOCK >= count), NEG, 0.0).astype(BF16)
        for h in range(heads):
            part = slice(h * HD, (h + 1) * HD)
            of_head = projected[3 * h * HD : 3 * (h + 1) * HD]
            query = ((of_head[:HD] + q_bias[part]).astype(BF16).astype(F32) * SCORE_SCALE).astype(BF16)
            keys = of_head[HD : 2 * HD].astype(BF16)
            values = (of_head[2 * HD :] + v_bias[part]).astype(BF16)
            r.query_t[i, h] = jnp.concatenate([query, one], axis=0)
            r.keys[h, here, :] = jnp.concatenate([keys, bias], axis=0).T
            r.values[h, here, :] = values.T
            r.keys_t[h, :, here] = keys
            r.values_t[h, :, here] = values

    @pl.loop(0, 2)
    def _(turn):
        units = [(block_of(2 * turn + place), h) for place in range(2) for h in range(heads)]
        scores = [dot(r.keys[h], r.query_t[block, h]) for block, h in units]
        for (block, h), score in zip(units, scores):
            peak = jnp.max(score, axis=0, keepdims=True)
            exped = jnp.exp(score - peak)
            total = jnp.sum(exped, axis=0, keepdims=True)
            exped = exped.astype(BF16)
            inverse = 1.0 / total
            r.exped[block, h] = exped
            r.inverse_total[block, h] = inverse
            mixed = dot(r.values_t[h], exped) * inverse
            r.mixed_t[block, pl.ds(pl.multiple_of(m * cols + h * HD, HD), HD), :] = mixed.astype(BF16)
        for place in range(2):
            mx_copy(1, turn, place).start()
            mx_copy(0, turn, place).start()

    for name in second:
        load(name).wait()
    slot = lax.broadcasted_iota(jnp.int32, (BLOCK, width), 0)
    r.key_acc[...] = jnp.zeros_like(r.key_acc)
    r.value_acc[...] = jnp.zeros_like(r.value_acc)

    @pl.loop(0, blocks)
    def _(i):
        here = rows_at(i * BLOCK, BLOCK)
        grad = r.og[here, :]
        grad = jnp.where(slot + i * BLOCK < count, grad.astype(F32), 0.0).astype(BF16)
        r.og[here, :] = grad
        r.hidden_grad[here, :] = dot_nt(grad, r.down[...])

    def mx_forward(turn):
        for place in range(2):
            mx_copy(1, turn, place).wait_recv()
            mx_copy(2, turn, place).start()

    def mx_arrive(kind, turn):
        for place in range(2):
            mx_copy(kind, turn, place).wait_recv()

    ow_copy(1).wait_recv()
    ow_copy(2).start()
    mx_forward(0)
    mx_arrive(0, 1)
    ow_copy(0).wait_recv()
    ow_copy(2).wait_recv()
    mx_arrive(2, 0)

    o_bias = row_of(r.o_bias)
    gain_two, shift_two = row_of(r.gain_two), row_of(r.shift_two)
    up_bias, down_bias = row_of(r.up_bias), row_of(r.down_bias)

    def feed_forward(pair, between):
        places = [rows_at(block_of(k) * BLOCK, BLOCK) for k in pair]
        attended = [dot_tn(r.mixed_t[block_of(k)], r.ow[...]) for k in pair]
        between()
        normed_two = []
        for k, here, value in zip(pair, places, attended):
            resid = r.feats[here, :].astype(F32) + (value + o_bias)
            std_rows, inverse = standardized(resid)
            if k == 0:
                r.resid[...] = resid
                r.std_two[...] = std_rows
                r.inverse_two[...] = inverse
            normed_two.append((std_rows * gain_two + shift_two).astype(BF16))
            r.normed_two[here, :] = normed_two[-1]
        pre_up = [dot(value, r.up[...]) + up_bias for value in normed_two]
        pre_grads = []
        for here, value in zip(places, pre_up):
            hidden, slope = gelu_pair(value)
            r.hidden[here, :] = hidden.astype(BF16)
            pre_grads.append((r.hidden_grad[here, :] * slope).astype(BF16))
            r.pre_grad[here, :] = pre_grads[-1]
        return pre_grads

    def feed_forward_out(k):
        return dot(r.hidden[rows_at(block_of(k) * BLOCK, BLOCK), :], r.down[...])

    pre_grads = feed_forward((3, 2), lambda: None)
    mx_forward(1)
    r.bk_tx[0] = dot_nt(pre_grads[0], r.up[...]).astype(BF16)
    rs_copy(BK, 0).start()
    r.back[...] = dot_nt(pre_grads[1], r.up[...])

    def send_back():
        rs_copy(BK, 0).wait_recv()
        r.bk_tx[1] = (r.back[...] + r.bk_rx[0].astype(F32)).astype(BF16)
        rs_copy(BK, 1).start()

    mx_arrive(0, 0)
    mx_arrive(2, 1)
    pre_grads = feed_forward((1, 0), send_back)

    def grad_tiles(left, right, pieces):
        right_all = right[...]

        @pl.loop(0, 2)
        def _(t):
            value = dot_tn(left[:, rows_at(t * 384, 384)], right_all)
            store_piece(pieces[0], t, value[:, :384])
            store_piece(pieces[1], t, value[:, 384:])

        dp_start(*pieces)

    grad_tiles(r.og, r.hidden, (DOWN0, DOWN1))
    grad_tiles(r.normed_two, r.pre_grad, (UP0, UP1))

    r.ml_tx[0] = feed_forward_out(3).astype(BF16)
    rs_copy(ML, 0).start()
    ml_x = feed_forward_out(2)
    r.bk_tx[2] = dot_nt(r.pre_grad[rows_at(block_of(1) * BLOCK, BLOCK), :], r.up[...]).astype(BF16)
    rs_copy(BK, 2).start()
    rs_copy(ML, 0).wait_recv()
    r.ml_tx[1] = (ml_x + r.ml_rx[0].astype(F32)).astype(BF16)
    ml_x_copy(0).start()
    r.back[...] = dot_nt(r.pre_grad[own, :], r.up[...])
    r.ml_tx[2] = feed_forward_out(1).astype(BF16)
    rs_copy(ML, 2).start()
    r.ml_own[...] = feed_forward_out(0)
    ones = jnp.ones((8, rows), BF16)
    r.small[6:7, :] = dot(ones, r.pre_grad[...])[:1]

    rs_copy(BK, 2).wait_recv()
    rs_copy(BK, 1).wait_recv()
    back = r.back[...] + r.bk_rx[2].astype(F32) + r.bk_rx[1].astype(F32)
    std_rows, inverse = r.std_two[...], r.inverse_two[...]
    own_grad = r.og[own, :].astype(F32)
    resid_grad = own_grad + norm_back(std_rows, inverse, gain_two, back)
    resid_low = resid_grad.astype(BF16)
    for k in (2, 3, 1):
        target_heads = r.ow[pl.ds(pl.multiple_of(mp_peers[k] * cols, 64), cols), :]
        r.mg_tx[k - 1] = dot_nt(target_heads, resid_low).astype(BF16)
        mg_copy(k).start()
    r.mixed_grad_t[m] = dot_nt(r.ow[own_heads, :], resid_low).astype(BF16)
    r.resid_grad[...] = resid_grad
    r.resid_low[c] = resid_low
    rl_copy().start()
    r.back[...] = back

    def attend_back(block):
        for h in range(heads):
            part = slice(h * HD, (h + 1) * HD)
            exped = r.exped[block, h]
            scaled = (r.mixed_grad_t[block, part, :].astype(F32) * r.inverse_total[block, h]).astype(BF16)
            mixed = r.mixed_t[block, pl.ds(pl.multiple_of(m * cols + h * HD, HD), HD), :]
            inner_product = column_sum(scaled.astype(F32) * mixed.astype(F32))
            prob_grad = dot(r.values[h], scaled)
            score_grad = (exped.astype(F32) * (prob_grad - inner_product)).astype(BF16)
            r.value_acc[h] += dot_nt(scaled, exped)
            r.key_acc[h] += dot_nt(r.query_t[block, h][:HD], score_grad)
            query_grad = dot(r.keys_t[h], score_grad) * SCORE_SCALE
            r.dqkv_t[3 * h * HD : (3 * h + 1) * HD, rows_at(block * BLOCK, BLOCK)] = query_grad.astype(BF16)

    def out_partial(head_rows):
        value = dot(r.mixed_t[m, head_rows, :], r.resid_low[c])
        return value + dot(r.mixed_t[cp, head_rows, :], r.resid_low[1 - c])

    @pl.loop(0, blocks)
    def _(i):
        @pl.when(i == 1)
        def _():
            poll(0)
            mg_copy(1).wait_recv()
            rl_copy().wait_recv()
            r.go_tx[...] = out_partial(pl.ds(pl.multiple_of(xp * cols, 64), cols)).astype(BF16)
            go_copy().start()
            ml_x_copy(1).start()

        @pl.when(i == 2)
        def _():
            poll(1)
            mg_copy(2).wait_recv()

        @pl.when(i == 3)
        def _():
            poll(2)
            mg_copy(3).wait_recv()

        attend_back(block_of(i))

    poll(3)

    for h in range(heads):
        row = 3 * h * HD
        r.dqkv_t[row + HD : row + 2 * HD, :] = r.key_acc[h].astype(BF16)
        r.dqkv_t[row + 2 * HD : row + 3 * HD, :] = r.value_acc[h].astype(BF16)
    value = dot(r.dqkv_t[...], r.normed[...])
    if dp_bits:
        value = value.astype(BF16)
    for t in range(2):
        for h in range(heads):
            store_piece(HEAD0 + h, t, value[h * cols : (h + 1) * cols, t * 384 : (t + 1) * 384].T)
    dp_start(HEAD0, HEAD1, HEAD2)
    poll(4)

    for step in range(3):
        rs_copy(BK, step).wait_send()
    r.gain_sum[...] = jnp.zeros_like(r.gain_sum)
    r.shift_sum[...] = jnp.zeros_like(r.shift_sum)

    def input_block(i):
        here = rows_at(block_of(3 - i) * BLOCK, BLOCK)
        part = dot_tn(r.dqkv_t[:, here], r.wqkv[...].reshape(3 * cols, width))

        @pl.when(i == 0)
        def _():
            r.bk_tx[0] = part.astype(BF16)
            rs_copy(IN, 0).start()

        @pl.when(i == 1)
        def _():
            rs_copy(IN, 0).wait_recv()
            r.bk_tx[1] = (part + r.in_rx[0].astype(F32)).astype(BF16)
            rs_copy(IN, 1).start()

        @pl.when(i == 2)
        def _():
            r.bk_tx[2] = part.astype(BF16)
            rs_copy(IN, 2).start()

        @pl.when(i == 3)
        def _():
            r.back[...] = part

        r.gain_sum[...] += column_sum(part * r.std_one[here, :].astype(F32))
        r.shift_sum[...] += column_sum(part)

    @pl.loop(0, 2)
    def _(i):
        input_block(i)

    poll(5)

    go_copy().wait_recv()
    value = out_partial(own_heads) + r.go_rx[...].astype(F32)
    for t in range(2):
        store_piece(OUT, t, value[:, t * 384 : (t + 1) * 384].T)
    dp_start(OUT)
    poll(6)

    r.small[2:3, :] = column_sum(r.resid_low[c].astype(F32))
    r.small[3:4, :] = column_sum(r.back[...] * r.std_two[...])
    r.small[4:5, :] = column_sum(r.back[...])
    r.small[5:6, :] = column_sum(r.og[own, :].astype(F32))

    @pl.loop(0, 2)
    def _(i):
        input_block(i + 2)

    poll(7)

    r.small[0:1, :] = r.gain_sum[...]
    r.small[1:2, :] = r.shift_sum[...]
    bias_sums = dot_nt(jnp.ones((8, rows), BF16), r.dqkv_t[...])[:1]
    q_sums = jnp.concatenate([bias_sums[:, 3 * h * HD : (3 * h + 1) * HD] for h in range(heads)], axis=1)
    v_sums = jnp.concatenate([bias_sums[:, (3 * h + 2) * HD : 3 * (h + 1) * HD] for h in range(heads)], axis=1)
    if dp_bits:
        dp_size = 1 << dp_bits
        share, head_share = width // dp_size, cols // dp_size
        blank = jnp.zeros((1, 128 - 2 * head_share), F32)
        for peer in range(dp_size):
            r.small_tx[peer, 0:7, :share] = r.small[0:7, peer * share : (peer + 1) * share]
            of_peer = slice(peer * head_share, (peer + 1) * head_share)
            r.small_tx[peer, 7:8, :] = jnp.concatenate([q_sums[:, of_peer], v_sums[:, of_peer], blank], axis=1)
        for k in range(1, dp_size):
            sd_copy(k).start()
    else:
        r.small[7:8, :] = jnp.concatenate([q_sums, v_sums, jnp.zeros((1, width - 2 * cols), F32)], axis=1)

    poll(8)
    ml_x_copy(0).wait_recv()
    ml_x_copy(1).wait_recv()
    rs_copy(ML, 2).wait_recv()
    mlp = r.ml_own[...] + r.ml_rx[2].astype(F32) + r.ml_rx[1].astype(F32)
    r.layer_out_v[...] = (r.resid[...] + (mlp + down_bias)).astype(BF16)
    write_out(0).start()
    std_rows, inverse = standardized(r.feats[own, :].astype(F32))
    poll(9)

    if dp_bits:
        total = r.small_tx[lax.axis_index(DP)]
        for k in range(1, 1 << dp_bits):
            sd_copy(k).wait_recv()
            total = total + r.sd_rx[k - 1]
        r.small_dp[...] = total
    else:
        r.small_dp[...] = r.small[...]
    for k in mp_peers:
        sg_copy(k).start()

    poll(10)
    rs_copy(IN, 2).wait_recv()
    rs_copy(IN, 1).wait_recv()
    back = r.back[...] + r.in_rx[2].astype(F32) + r.in_rx[1].astype(F32)
    r.feats_grad_v[...] = (r.resid_grad[...] + norm_back(std_rows, inverse, gain_one, back)).astype(BF16)
    write_out(1).start()

    total = r.small_dp[...]
    for k in mp_peers:
        sg_copy(k).wait_recv()
        of_peer = r.sg_rx[k - 1]
        total = total + jnp.where(lax.broadcasted_iota(jnp.int32, of_peer.shape, 0) < 6, of_peer, 0.0)
    r.small_out_v[...] = total
    write_out(2).start()
    poll(11)
    if not dp_bits:
        for piece in range(len(PLANS)):
            write_out(3 + piece).start()

    for i in range(len(done)):
        write_out(i).wait()
    for kind in range(3):
        ow_copy(kind).wait_send()
        rs_copy(IN, kind).wait_send()
        for turn in range(2):
            for place in range(2):
                mx_copy(kind, turn, place).wait_send()
    rl_copy().wait_send()
    go_copy().wait_send()
    rs_copy(ML, 0).wait_send()
    rs_copy(ML, 2).wait_send()
    ml_x_copy(0).wait_send()
    ml_x_copy(1).wait_send()
    for k in mp_peers:
        mg_copy(k).wait_send()
        sg_copy(k).wait_send()
    if dp_bits:
        for k in range(1, 1 << dp_bits):
            sd_copy(k).wait_send()
        for piece, plan in enumerate(PLANS):
            for stage in range(len(ARRIVING[plan])):
                each(piece, stage, leave)


def finish_kernel(names, *refs):
    r = types.SimpleNamespace(**dict(zip(names, refs)))
    grads = refs[len(names) :]
    shard = r.up.shape[0]
    unpacked = (r.head0, r.head1, r.head2, r.o)
    incoming = [
        (r.small_out, r.small), (r.layer_out, r.layer), (r.feats_grad, r.feats), *zip(grads[HEAD0:], unpacked),
        (grads[UP0], r.up.at[:, pl.ds(0, 384)]), (grads[UP1], r.up.at[:, pl.ds(384, 384)]),
        (grads[DOWN0], r.down.at[:, pl.ds(0, 384)]), (grads[DOWN1], r.down.at[:, pl.ds(384, 384)]),
    ]
    outgoing = [
        (r.layer, r.out_layer), (r.feats, r.out_feats), (r.up, r.out_up), (r.down, r.out_down), (r.q, r.out_q),
        (r.k, r.out_k), (r.v, r.out_v), (r.o_t, r.out_o), (r.up_bias, r.out_up_bias),
    ]
    vectors = (r.out_gain_one, r.out_shift_one, r.out_o_bias, r.out_gain_two, r.out_shift_two, r.out_down_bias, r.out_q_bias,
               r.out_v_bias)
    outgoing += [(r.pieces.at[i], target) for i, target in enumerate(vectors)]

    def take(i):
        return pltpu.make_async_copy(*incoming[i], r.in_sem.at[i])

    def give(i):
        return pltpu.make_async_copy(*outgoing[i], r.out_sem.at[i])

    for i in range(len(incoming)):
        take(i).start()
    take(0).wait()
    m = lax.axis_index(MP)
    small = r.small[...]
    piece = r.out_gain_one.shape[0]
    mine = pltpu.roll(small, (128 - m * piece) % 128, 1)
    for i in range(6):
        r.pieces[i] = mine[i, :piece]
    r.pieces[6] = small[7, :piece]
    r.pieces[7] = small[7, piece : 2 * piece]
    r.up_bias[...] = small[6, :shard]
    for i in range(8, len(outgoing)):
        give(i).start()
    for i in (1, 2):
        take(i).wait()
        give(i - 1).start()
    for i in range(3, 7):
        take(i).wait()
    heads = [jnp.concatenate([ref[:, :192], ref[:, 192:]], axis=0) for ref in unpacked]
    for i, target in enumerate((r.q, r.k, r.v)):
        target[...] = jnp.concatenate([value[:, i * HD : (i + 1) * HD] for value in heads[:3]], axis=1)
        give(4 + i).start()
    r.o_t[...] = heads[3].T
    give(7).start()
    for i in range(7, 11):
        take(i).wait()
        if i % 2 == 0:
            give((i - 4) // 2).start()
    for i in range(len(outgoing)):
        give(i).wait()


def layer_call(dp_size, clip_feats, counts, gain_one, shift_one, q_weight, k_weight, v_weight, q_bias, v_bias, o_weight,
               o_bias, gain_two, shift_two, up_weight, up_bias, down_weight, down_bias, out_grad):
    rows, width = clip_feats.shape
    cols = q_weight.shape[1]
    heads = cols // HD
    hidden_cols = up_weight.shape[1]
    dp_bits = 3 if dp_size == 8 else 0
    vmem = pl.BlockSpec(memory_space=pltpu.VMEM)
    anywhere = pl.BlockSpec(memory_space=pl.ANY)
    by_head = (heads, HD, width)
    inputs = dict(
        gain_one_hbm=(gain_one, anywhere), shift_one_hbm=(shift_one, anywhere), q_bias_hbm=(q_bias, anywhere),
        v_bias_hbm=(v_bias, anywhere), o_bias_hbm=(o_bias, anywhere), gain_two_hbm=(gain_two, anywhere),
        shift_two_hbm=(shift_two, anywhere), up_bias_hbm=(up_bias, anywhere),
        down_bias_hbm=(down_bias, anywhere), counts_hbm=(counts, anywhere),
        feats_hbm=(clip_feats, anywhere), qw_hbm=(q_weight.T.reshape(by_head), anywhere),
        kw_hbm=(k_weight.T.reshape(by_head), anywhere), vw_hbm=(v_weight.T.reshape(by_head), anywhere),
        ow_hbm=(o_weight, anywhere), up_hbm=(up_weight, anywhere),
        down_hbm=(down_weight, anywhere), og_hbm=(out_grad, anywhere),
    )
    shard = width // dp_size if dp_bits else width
    small_shape = (8, 128) if dp_bits else (8, width)
    outputs = dict(layer_out=((BLOCK, width), BF16), feats_grad=((BLOCK, width), BF16), small_out=(small_shape, F32))
    grads = [(packed_shape(i, shard) if dp_bits else (width, COLUMNS[i]), F32) for i in range(len(PLANS))]
    piece = (BLOCK, width)
    scratch = dict(
        gain_one=((width,), BF16), shift_one=((width,), BF16), q_bias=((cols,), BF16), v_bias=((cols,), BF16),
        o_bias=((width,), BF16), gain_two=((width,), BF16), shift_two=((width,), BF16),
        up_bias=((hidden_cols,), BF16), down_bias=((width,), BF16),
        feats=((rows, width), BF16), wqkv=((heads, 3 * HD, width), BF16), ow=((width, width), BF16),
        og=((rows, width), BF16), down=((hidden_cols, width), BF16), up=((width, hidden_cols), BF16),
        normed=((rows, width), BF16), std_one=((rows, width), BF16),
        query_t=((rows // BLOCK, heads, 2 * HD, BLOCK), BF16), keys=((heads, rows, 2 * HD), BF16), values=((heads, rows, HD), BF16),
        keys_t=((heads, HD, rows), BF16), values_t=((heads, HD, rows), BF16), mixed_t=((rows // BLOCK, width, BLOCK), BF16),
        exped=((rows // BLOCK, heads, rows, BLOCK), BF16), inverse_total=((rows // BLOCK, heads, 1, BLOCK), F32), hidden_grad=((rows, hidden_cols), F32), resid=(piece, F32),
        normed_two=((rows, width), BF16), hidden=((rows, hidden_cols), BF16), pre_grad=((rows, hidden_cols), BF16),
        back=(piece, F32), resid_grad=(piece, F32),
        resid_low=((2,) + piece, BF16), go_tx=((cols, width), BF16), go_rx=((cols, width), BF16), std_two=(piece, F32), inverse_two=((BLOCK, 1), F32), ml_own=(piece, F32),
        bk_tx=((3,) + piece, BF16), bk_rx=((3,) + piece, BF16), ml_tx=((3,) + piece, BF16),
        ml_rx=((3,) + piece, BF16), in_rx=((3,) + piece, BF16),
        mg_tx=((3, cols, BLOCK), BF16), mixed_grad_t=((rows // BLOCK, cols, BLOCK), BF16),
        key_acc=((heads, HD, rows), F32), value_acc=((heads, HD, rows), F32), dqkv_t=((3 * cols, rows), BF16),
        gain_sum=((1, width), F32), shift_sum=((1, width), F32),
        small=((8, width), F32), small_dp=(small_shape, F32), sg_rx=((3,) + small_shape, F32),
    )
    scratch.update({name + "_v": spec for name, spec in outputs.items()})
    of_pieces = list(grads)
    if dp_bits:
        scratch.update(
            small_tx=((dp_size,) + small_shape, F32), sd_rx=((dp_size - 1,) + small_shape, F32)
        )
        for table in (HELD, ARRIVING):
            for i, plan in enumerate(PLANS):
                of_pieces += [((count,) + packed_shape(i, shard), BF16) for count in table[plan]]
    copies = 29 + 12 + 4 * len(PLANS)
    scalars = dict(
        counts=pltpu.SMEM((1,), jnp.int32), load_sem=pltpu.SemaphoreType.DMA((17 + rows // BLOCK,)),
        out_sem=pltpu.SemaphoreType.DMA((len(outputs) + len(grads),)), send_sem=pltpu.SemaphoreType.DMA((copies,)),
        recv_sem=pltpu.SemaphoreType.DMA((copies,)),
    )
    names = list(inputs) + list(outputs)
    kernel_names = [*inputs, *outputs, *scratch, *scalars]

    def kernel(*refs):
        refs = list(refs)
        grad_refs = refs[len(names) : len(names) + len(grads)]
        rest = refs[len(names) + len(grads) :]
        named = len(scratch) + len(scalars)
        layer_kernel(kernel_names, dp_bits, *refs[: len(names)], *rest[:named], *grad_refs, *rest[named:])

    results = pl.pallas_call(
        kernel,
        out_shape=[jax.ShapeDtypeStruct(*spec) for spec in [*outputs.values(), *grads]],
        in_specs=[spec for _, spec in inputs.values()],
        out_specs=[anywhere] * (len(outputs) + len(grads)),
        scratch_shapes=[pltpu.VMEM(*spec) for spec in scratch.values()] + list(scalars.values())
        + [pltpu.VMEM(*spec) for spec in of_pieces],
        compiler_params=pltpu.CompilerParams(collective_id=0, has_side_effects=True, vmem_limit_bytes=67043328),
        name="layer",
    )(*[value for value, _ in inputs.values()])
    return dict(zip(outputs, results)), results[len(outputs) :]


def finish_call(out, grads, cols, hidden_cols):
    shard, width = COLUMNS[UP0] // 4, out["layer_out"].shape[1]
    rows = ((BLOCK, width), BF16)
    small = ((shard // 4,), F32)
    head = ((shard, cols), F32)
    shapes = dict(
        out_layer=rows, out_feats=rows, out_gain_one=small, out_shift_one=small, out_q=head, out_k=head, out_v=head,
        out_q_bias=small, out_v_bias=small, out_o=((cols, shard), F32), out_o_bias=small, out_gain_two=small,
        out_shift_two=small, out_up=((shard, hidden_cols), F32), out_up_bias=((shard,), F32),
        out_down=((shard, hidden_cols), F32), out_down_bias=small,
    )
    packed = (packed_shape(OUT, shard), F32)
    scratch = dict(
        small=((8, 128), F32), layer=rows, feats=rows, head0=packed, head1=packed, head2=packed, o=packed,
        up=((shard, hidden_cols), F32), down=((shard, hidden_cols), F32), q=head, k=head, v=head, o_t=((cols, shard), F32),
        up_bias=((shard,), F32), pieces=((8, shard // 4), F32),
    )
    sems = dict(in_sem=pltpu.SemaphoreType.DMA((11,)), out_sem=pltpu.SemaphoreType.DMA((17,)))
    names = [*out, *shapes, *scratch, *sems]

    def kernel(*refs):
        count = len(out) + len(grads)
        finish_kernel(names, *refs[: len(out)], *refs[count:], *refs[len(out) : count])

    anywhere = pl.BlockSpec(memory_space=pl.ANY)
    results = pl.pallas_call(
        kernel,
        out_shape=[jax.ShapeDtypeStruct(*spec) for spec in shapes.values()],
        in_specs=[anywhere] * (len(out) + len(grads)),
        out_specs=[anywhere] * len(shapes),
        scratch_shapes=[pltpu.VMEM(*spec) for spec in scratch.values()] + list(sems.values()),
        name="finish",
    )(*out.values(), *grads)
    return (*results[:15], results[15].T, results[16])


def shards(dp_size, *args):
    out, grads = layer_call(dp_size, *args)
    cols, hidden_cols = args[4].shape[1], args[13].shape[1]
    if dp_size == 8:
        return finish_call(out, grads, cols, hidden_cols)

    def over(value, dim):
        return lax.psum_scatter(value, DP, scatter_dimension=dim, tiled=True)

    small = lax.psum(out["small_out"], DP)
    width = small.shape[1]
    d, m = lax.axis_index(DP), lax.axis_index(MP)
    piece = width // (dp_size * 4)
    group = [lax.dynamic_slice(small, (i, (d * 4 + m) * piece), (1, piece)).reshape(piece) for i in range(6)]
    up_piece = hidden_cols // dp_size
    head_piece = cols // dp_size
    up_bias = lax.dynamic_slice(small, (6, d * up_piece), (1, up_piece)).reshape(up_piece)
    q_bias = lax.dynamic_slice(small, (7, d * head_piece), (1, head_piece)).reshape(head_piece)
    v_bias = lax.dynamic_slice(small, (7, cols + d * head_piece), (1, head_piece)).reshape(head_piece)
    heads = grads[HEAD0 : HEAD2 + 1]
    q_grad, k_grad, v_grad = (
        jnp.concatenate([value[:, i * HD : (i + 1) * HD] for value in heads], axis=1) for i in range(3)
    )
    up_grad = jnp.concatenate([grads[UP0], grads[UP1]], axis=1)
    down_grad = jnp.concatenate([grads[DOWN0], grads[DOWN1]], axis=1)
    return (
        out["layer_out"], out["feats_grad"], group[0], group[1], over(q_grad, 0), over(k_grad, 0), over(v_grad, 0),
        q_bias, v_bias, over(grads[OUT].T, 1), group[2], group[3], group[4], over(up_grad, 0), up_bias,
        over(down_grad.T, 1), group[5],
    )


def solution(mesh):
    placed = (
        P(DP, None), P(DP), P(), P(), P(None, MP), P(None, MP), P(None, MP), P(MP), P(MP), P(MP, None),
        P(), P(), P(), P(None, MP), P(MP), P(MP, None), P(), P(DP, None),
    )
    return jax.shard_map(
        functools.partial(shards, mesh.shape[DP]),
        mesh=mesh,
        in_specs=placed,
        out_specs=(
            P((DP, MP), None), P((DP, MP), None), P((DP, MP)), P((DP, MP)), P(DP, MP), P(DP, MP),
            P(DP, MP), P((MP, DP)), P((MP, DP)), P(MP, DP), P((DP, MP)), P((DP, MP)),
            P((DP, MP)), P(DP, MP), P((MP, DP)), P(MP, DP), P((DP, MP)),
        ),
        check_vma=False,
    )
```

time: 109 us -> 79.3 us (0.73)
  Pallas kernels: 92.8 us -> 77.6 us
  local copies, waits for them, and re-layouts: 14.1 us -> 0 us
    pallas_call x1 -> x2, Pallas kernels: 92.8 us -> 77.6 us  [the longest x1 75.1 us: layer_call(): pl.pallas_call(kernel, out_shape=[jax.ShapeDtypeStruct(*spec) for spec in...]
    unnamed x16 -> x0, local copies, waits for them, and re-layouts: 9.38 us -> none
    reshape x2 -> x0, local copies, waits for them, and re-layouts: 2.86 us -> none  [the longest x1 1.58 us: shards(): lax.dynamic_slice(small, (i, (d * 4 + m) * piece), (1, piece))]
    transpose x1 -> x0, local copies, waits for them, and re-layouts: 1.83 us -> none  [shards(): g_vo[:, cols:]]
where the time goes in v2:
time: 79.3 us; the launch traced here: 79.1 us
  Pallas kernels  77.6 us (98%)
  between operations  1.48 us (2%)
    pallas_call x1, Pallas kernels, layer_call(): pl.pallas_call(kernel, out_shape=[jax.ShapeDtypeStruct(*spec) for spec in...  75.1 us
    pallas_call x1, Pallas kernels, finish_call(): pl.pallas_call(kernel, out_shape=[jax.ShapeDtypeStruct(*spec) for spec in...  2.57 us

profile of v2, /device:TPU:0, one launch (start us, length us, event | category | flops | bytes accessed | tf_op | source)
XLA Modules:
  0.0 79.1 jit_solution(7247062028509544448)
XLA Ops:
  1.3 75.1 %layer.1 = (bf16[256,768]{1,0:T(8,128)(2,1)}, bf16[256,768]{1,0:T(8,128)(2,1)}, f32[8,128]{1,0:T(8,128)}, f32[96,384]{1,0:T(8,128)}, f32[96,384]{1,0:T(8,128)}, ...) custom-call(bf16[768]{0:T(1024)(128)(2,1)} %refs_0_.1, ...), custom_call_target="tpu_custom_call" | custom-call | tf_op jit(solution)/shard_map/layer/pallas_call | solution.py:861
  76.4 2.6 %finish.1 = (bf16[256,768]{1,0:T(8,128)(2,1)}, bf16[256,768]{1,0:T(8,128)(2,1)}, f32[24]{0:T(128)}, f32[24]{0:T(128)}, f32[96,192]{1,0:T(8,128)}, /*index=5*/f32...) custom-call(bf16[256,768]{1,0:T(8,128)(2,1)} %get-tuple-element.45.r, ...), custom_call_target="tpu_custom_call" | custom-call | tf_op jit(solution)/shard_map/finish/pallas_call | solution.py:899

commit v3 on v2

--- a/solution.py
+++ b/solution.py
@@ -32,15 +32,15 @@
 POLLS = (
     ((DOWN0, 0), (DOWN1, 0)),
     (),
+    ((UP0, 0),),
+    ((DOWN0, 1),),
+    ((DOWN1, 1),),
+    ((UP1, 0),),
+    ((DOWN0, 2), (UP0, 1)),
     (),
-    ((UP0, 0), (DOWN0, 1)),
-    ((DOWN1, 1),),
-    (),
-    ((UP1, 0), (DOWN0, 2)),
-    ((UP0, 1),),
-    ((DOWN1, 2), (UP1, 1), (HEAD0, 0)),
-    ((UP0, 2), (DOWN0, 3), (HEAD1, 0), (UP1, 2), (HEAD2, 0), (OUT, 0)),
-    ((UP0, 3), (DOWN1, 3), (HEAD0, 1), (HEAD1, 1), (HEAD2, 1), (OUT, 1), (UP1, 3)),
+    ((HEAD0, 0), (DOWN1, 2), (UP1, 1)),
+    ((HEAD1, 0), (UP0, 2), (DOWN0, 3), (HEAD0, 1), (HEAD2, 0), (UP1, 2)),
+    ((HEAD1, 1), (OUT, 0), (UP0, 3), (DOWN1, 3), (HEAD2, 1), (UP1, 3), (OUT, 1)),
     ((HEAD0, 2), (HEAD1, 2), (HEAD2, 2), (OUT, 2)),
 )
 
@@ -192,10 +192,6 @@
     def rs_copy(base, step):
         send, receive = {BK: (r.bk_tx, r.bk_rx), ML: (r.ml_tx, r.ml_rx), IN: (r.bk_tx, r.in_rx)}[base]
         return remote(base + step, send.at[step], receive.at[step], {MP: (cp, xp, cp)[step]})
-
-    def ml_x_copy(half):
-        part = pl.ds(half * (BLOCK // 2), BLOCK // 2)
-        return remote((ML + 1, ML + 3)[half], r.ml_tx.at[1, part], r.ml_rx.at[1, part], {MP: xp})
 
     def mg_copy(k):
         return remote(MG + k - 1, r.mg_tx.at[k - 1], r.mixed_grad_t.at[m], {MP: mp_peers[k]})
@@ -476,9 +472,9 @@
         return dot(r.hidden[rows_at(block_of(k) * BLOCK, BLOCK), :], r.down[...])
 
     pre_grads = feed_forward((3, 2), lambda: None)
-    mx_forward(1)
     r.bk_tx[0] = dot_nt(pre_grads[0], r.up[...]).astype(BF16)
     rs_copy(BK, 0).start()
+    mx_forward(1)
     r.back[...] = dot_nt(pre_grads[1], r.up[...])
 
     def send_back():
@@ -511,7 +507,6 @@
     rs_copy(BK, 2).start()
     rs_copy(ML, 0).wait_recv()
     r.ml_tx[1] = (ml_x + r.ml_rx[0].astype(F32)).astype(BF16)
-    ml_x_copy(0).start()
     r.back[...] = dot_nt(r.pre_grad[own, :], r.up[...])
     r.ml_tx[2] = feed_forward_out(1).astype(BF16)
     rs_copy(ML, 2).start()
@@ -563,7 +558,7 @@
             rl_copy().wait_recv()
             r.go_tx[...] = out_partial(pl.ds(pl.multiple_of(xp * cols, 64), cols)).astype(BF16)
             go_copy().start()
-            ml_x_copy(1).start()
+            rs_copy(ML, 1).start()
 
         @pl.when(i == 2)
         def _():
@@ -624,14 +619,13 @@
         r.gain_sum[...] += column_sum(part * r.std_one[here, :].astype(F32))
         r.shift_sum[...] += column_sum(part)
 
-    @pl.loop(0, 2)
-    def _(i):
-        input_block(i)
-
+    input_block(0)
+    partial = out_partial(own_heads)
+    input_block(1)
     poll(5)
 
     go_copy().wait_recv()
-    value = out_partial(own_heads) + r.go_rx[...].astype(F32)
+    value = partial + r.go_rx[...].astype(F32)
     for t in range(2):
         store_piece(OUT, t, value[:, t * 384 : (t + 1) * 384].T)
     dp_start(OUT)
@@ -667,8 +661,7 @@
         r.small[7:8, :] = jnp.concatenate([q_sums, v_sums, jnp.zeros((1, width - 2 * cols), F32)], axis=1)
 
     poll(8)
-    ml_x_copy(0).wait_recv()
-    ml_x_copy(1).wait_recv()
+    rs_copy(ML, 1).wait_recv()
     rs_copy(ML, 2).wait_recv()
     mlp = r.ml_own[...] + r.ml_rx[2].astype(F32) + r.ml_rx[1].astype(F32)
     r.layer_out_v[...] = (r.resid[...] + (mlp + down_bias)).astype(BF16)
@@ -711,15 +704,12 @@
     for kind in range(3):
         ow_copy(kind).wait_send()
         rs_copy(IN, kind).wait_send()
+        rs_copy(ML, kind).wait_send()
         for turn in range(2):
             for place in range(2):
                 mx_copy(kind, turn, place).wait_send()
     rl_copy().wait_send()
     go_copy().wait_send()
-    rs_copy(ML, 0).wait_send()
-    rs_copy(ML, 2).wait_send()
-    ml_x_copy(0).wait_send()
-    ml_x_copy(1).wait_send()
     for k in mp_peers:
         mg_copy(k).wait_send()
         sg_copy(k).wait_send()

time: 79.3 us -> 77.9 us (0.982)
  Pallas kernels: 77.6 us -> 76 us
    pallas_call x1, Pallas kernels: 75.1 us -> 73.4 us  [layer_call(): pl.pallas_call(kernel, out_shape=[jax.ShapeDtypeStruct(*spec) for spec in...]
where the time goes in v3:
time: 77.9 us; the launch traced here: 77.4 us
  Pallas kernels  76 us (98%)
  between operations  1.48 us (2%)
    pallas_call x1, Pallas kernels, layer_call(): pl.pallas_call(kernel, out_shape=[jax.ShapeDtypeStruct(*spec) for spec in...  73.4 us
    pallas_call x1, Pallas kernels, finish_call(): pl.pallas_call(kernel, out_shape=[jax.ShapeDtypeStruct(*spec) for spec in...  2.57 us

profile of v3, /device:TPU:0, one launch (start us, length us, event | category | flops | bytes accessed | tf_op | source)
XLA Modules:
  0.0 77.4 jit_solution(16833164117170335034)
XLA Ops:
  1.3 73.4 %layer.1 = (bf16[256,768]{1,0:T(8,128)(2,1)}, bf16[256,768]{1,0:T(8,128)(2,1)}, f32[8,128]{1,0:T(8,128)}, f32[96,384]{1,0:T(8,128)}, f32[96,384]{1,0:T(8,128)}, ...) custom-call(bf16[768]{0:T(1024)(128)(2,1)} %refs_0_.1, ...), custom_call_target="tpu_custom_call" | custom-call | tf_op jit(solution)/shard_map/layer/pallas_call | solution.py:851
  74.7 2.6 %finish.1 = (bf16[256,768]{1,0:T(8,128)(2,1)}, bf16[256,768]{1,0:T(8,128)(2,1)}, f32[24]{0:T(128)}, f32[24]{0:T(128)}, f32[96,192]{1,0:T(8,128)}, /*index=5*/f32...) custom-call(bf16[256,768]{1,0:T(8,128)(2,1)} %get-tuple-element.45.r, ...), custom_call_target="tpu_custom_call" | custom-call | tf_op jit(solution)/shard_map/finish/pallas_call | solution.py:889

commit v4 on v3

--- a/solution.py
+++ b/solution.py
@@ -23,7 +23,7 @@
 YN, NY, YD, ZYZ, YZZ = range(5)
 HALVED = {ZYZ: (1, 0, 2), YZZ: (0, 1, 2)}
 DOWN0, DOWN1, UP0, UP1, HEAD0, HEAD1, HEAD2, OUT = range(8)
-PLANS = (YN, NY, YN, YN, YZZ, YZZ, YZZ, YZZ)
+PLANS = (YZZ, NY, YN, YZZ, YZZ, YZZ, YZZ, YZZ)
 COLUMNS = (384, 384, 384, 384, 192, 192, 192, 192)
 HELD = {YN: (8, 4, 2), NY: (8, 4, 2), YD: (8, 4), ZYZ: (8, 4, 2), YZZ: (8, 4, 2)}
 ARRIVING = {YN: (4, 2, 2, 1), NY: (4, 4, 2, 1), YD: (4, 3), ZYZ: (4, 2, 1), YZZ: (4, 2, 1)}
@@ -36,11 +36,11 @@
     ((DOWN0, 1),),
     ((DOWN1, 1),),
     ((UP1, 0),),
-    ((DOWN0, 2), (UP0, 1)),
+    ((UP0, 1),),
     (),
-    ((HEAD0, 0), (DOWN1, 2), (UP1, 1)),
-    ((HEAD1, 0), (UP0, 2), (DOWN0, 3), (HEAD0, 1), (HEAD2, 0), (UP1, 2)),
-    ((HEAD1, 1), (OUT, 0), (UP0, 3), (DOWN1, 3), (HEAD2, 1), (UP1, 3), (OUT, 1)),
+    ((HEAD0, 0), (DOWN1, 2), (UP1, 1), (DOWN0, 2)),
+    ((HEAD1, 0), (UP0, 2), (HEAD0, 1), (HEAD2, 0)),
+    ((HEAD1, 1), (OUT, 0), (UP0, 3), (DOWN1, 3), (HEAD2, 1), (UP1, 2), (OUT, 1)),
     ((HEAD0, 2), (HEAD1, 2), (HEAD2, 2), (OUT, 2)),
 )
 

time: 77.9 us -> 77.5 us (level)
  no operation moved by 1% of the time
where the time goes in v4:
time: 77.5 us; the launch traced here: 77.3 us
  Pallas kernels  75.8 us (98%)
  between operations  1.48 us (2%)
    pallas_call x1, Pallas kernels, layer_call(): pl.pallas_call(kernel, out_shape=[jax.ShapeDtypeStruct(*spec) for spec in...  73.2 us
    pallas_call x1, Pallas kernels, finish_call(): pl.pallas_call(kernel, out_shape=[jax.ShapeDtypeStruct(*spec) for spec in...  2.57 us

profile of v4, /device:TPU:0, one launch (start us, length us, event | category | flops | bytes accessed | tf_op | source)
XLA Modules:
  0.0 77.3 jit_solution(8236117702658731721)
XLA Ops:
  1.3 73.2 %layer.1 = (bf16[256,768]{1,0:T(8,128)(2,1)}, bf16[256,768]{1,0:T(8,128)(2,1)}, f32[8,128]{1,0:T(8,128)}, f32[96,384]{1,0:T(8,128)}, f32[96,384]{1,0:T(8,128)}, ...) custom-call(bf16[768]{0:T(1024)(128)(2,1)} %refs_0_.1, ...), custom_call_target="tpu_custom_call" | custom-call | tf_op jit(solution)/shard_map/layer/pallas_call | solution.py:851
  74.6 2.6 %finish.1 = (bf16[256,768]{1,0:T(8,128)(2,1)}, bf16[256,768]{1,0:T(8,128)(2,1)}, f32[24]{0:T(128)}, f32[24]{0:T(128)}, f32[96,192]{1,0:T(8,128)}, /*index=5*/f32...) custom-call(bf16[256,768]{1,0:T(8,128)(2,1)} %get-tuple-element.45.r, ...), custom_call_target="tpu_custom_call" | custom-call | tf_op jit(solution)/shard_map/finish/pallas_call | solution.py:889
